TPU v7x, 32 devices: a whole 2x2x4 slice. The times are simulated.
32 devices in a mesh: dp: 2 (over x), sub: 4 (over z), ep: 4 (over y, core).
Axes of the slice: x: 2, y: 2, z: 4, core: 2. Of those that a mesh axis runs over, the one named last changes fastest.
Arguments:
- input_a: bfloat16 [32, 256, 2048], P(('dp', 'ep', 'sub')), parts along dimension 0
- input_b: bfloat16 [32, 256, 2048], P(('dp', 'ep', 'sub')), parts along dimension 0
- route_idx: int32 [2, 8192, 8], P(None, ('dp', 'ep', 'sub')), parts along dimension 1
- route_gate: float32 [2, 8192, 8], P(None, ('dp', 'ep', 'sub')), parts along dimension 1
- attn_norm: float32 [2048], replicated
- w_query: bfloat16 [2048, 16, 128], replicated
- w_key: bfloat16 [2048, 16, 128], replicated
- w_value: bfloat16 [2048, 16, 128], replicated
- w_out: bfloat16 [16, 128, 2048], replicated
- moe_norm: float32 [2048], replicated
- w_gate: bfloat16 [64, 2048, 1024], P(('ep', 'sub'))
- w_up: bfloat16 [64, 2048, 1024], P(('ep', 'sub'))
- w_down: bfloat16 [64, 1024, 2048], P(('ep', 'sub'))
Outputs:
- output 1: bfloat16 [32, 256, 2048], P(('dp', 'ep', 'sub')), parts along dimension 0
- output 2: bfloat16 [32, 256, 2048], P(('dp', 'ep', 'sub')), parts along dimension 0
There are 2 independent parts. A program takes and returns all parts, laid end to end along the dimension named above; an argument that names none is the same for every part.
All inputs are finite; a program needn't handle non-finite values.
Results may differ from a plain program's by a relative error of at most 0.0132676.
Values are sent between devices in bfloat16 or wider.
A program may use at most 1 GiB of HBM per device.

v0:
```python
import jax
import jax.numpy as jnp
from jax import lax
from jax.sharding import PartitionSpec as P

NORM_EPS = 1e-6


def rms_norm(values, norm_gain):
    acc_f32 = values.astype(jnp.float32)
    inv_rms = lax.rsqrt(jnp.mean(acc_f32 * acc_f32, axis=-1, keepdims=True) + NORM_EPS)
    return (acc_f32 * inv_rms * norm_gain).astype(jnp.bfloat16)


def attention_block(tokens, attn_norm, w_query, w_key, w_value, w_out):
    normed = rms_norm(tokens, attn_norm)
    q_heads = jnp.einsum('bsd,dhc->bshc', normed, w_query, preferred_element_type=jnp.float32).astype(jnp.bfloat16)
    k_heads = jnp.einsum('bsd,dhc->bshc', normed, w_key, preferred_element_type=jnp.float32).astype(jnp.bfloat16)
    v_heads = jnp.einsum('bsd,dhc->bshc', normed, w_value, preferred_element_type=jnp.float32).astype(jnp.bfloat16)
    score_scale = w_query.shape[2] ** -0.5
    scores = jnp.einsum('bqhc,bkhc->bhqk', q_heads, k_heads, preferred_element_type=jnp.float32) * score_scale
    seq_len = tokens.shape[1]
    causal = lax.broadcasted_iota(jnp.int32, (seq_len, seq_len), 0) >= lax.broadcasted_iota(jnp.int32, (seq_len, seq_len), 1)
    scores = jnp.where(causal, scores, -jnp.inf)
    prob_bf = jax.nn.softmax(scores, axis=-1).astype(jnp.bfloat16)
    context = jnp.einsum('bhqk,bkhc->bqhc', prob_bf, v_heads, preferred_element_type=jnp.float32).astype(jnp.bfloat16)
    proj_out = jnp.einsum('crid,ide->cre', context, w_out, preferred_element_type=jnp.float32)
    return (tokens.astype(jnp.float32) + proj_out).astype(jnp.bfloat16)


def route_slots(exp_ids, num_exp, cap_slots):
    tok_count, top_k = exp_ids.shape
    flat_ids = exp_ids.reshape(-1)
    sort_order = jnp.argsort(flat_ids, stable=True)
    sorted_ids = flat_ids[sort_order]
    counts = jnp.bincount(flat_ids, length=num_exp)
    starts = jnp.cumsum(counts) - counts
    slot_rank = jnp.arange(flat_ids.shape[0], dtype=jnp.int32) - starts[sorted_ids]
    slot_sorted = sorted_ids * cap_slots + slot_rank
    slot_of = jnp.zeros_like(flat_ids).at[sort_order].set(slot_sorted)
    holder = jnp.full((num_exp * cap_slots,), tok_count, jnp.int32).at[slot_sorted].set(sort_order // top_k)
    return slot_of, holder


def expert_ffn(disp_rows, w_gate, w_up, w_down):
    gate_h = jnp.einsum('end,edf->enf', disp_rows, w_gate, preferred_element_type=jnp.float32)
    up_h = jnp.einsum('end,edf->enf', disp_rows, w_up, preferred_element_type=jnp.float32)
    act_rows = (jax.nn.silu(gate_h) * up_h).astype(jnp.bfloat16)
    return jnp.einsum('enf,efd->end', act_rows, w_down, preferred_element_type=jnp.float32).astype(jnp.bfloat16)


def micro_step(tokens, exp_ids, gate_w, attn_norm, w_query, w_key, w_value, w_out, moe_norm, w_gate, w_up, w_down, ep_size, sub_size):
    hidden = attention_block(tokens, attn_norm, w_query, w_key, w_value, w_out)
    seq_count, seq_len, model_dim = hidden.shape
    flat_tok = hidden.reshape(seq_count * seq_len, model_dim)
    tok_count, top_k = exp_ids.shape
    exp_local = w_gate.shape[0]
    num_exp = exp_local * ep_size * sub_size
    cap_slots = 3 * top_k * tok_count // (2 * num_exp)
    normed = rms_norm(flat_tok, moe_norm)
    slot_of, holder = route_slots(exp_ids, num_exp, cap_slots)
    send_buf = jnp.take(normed, holder, axis=0, mode='fill', fill_value=0)
    send_buf = send_buf.reshape(ep_size, sub_size, exp_local, cap_slots, model_dim)
    across_ep = lax.all_to_all(send_buf, 'ep', 0, 3, tiled=True)
    arrived = lax.all_to_all(across_ep, 'sub', 1, 3, tiled=True)
    expert_out = expert_ffn(arrived.reshape(exp_local, -1, model_dim), w_gate, w_up, w_down)
    back_sub = lax.all_to_all(expert_out.reshape(1, 1, exp_local, -1, model_dim), 'sub', 3, 1, tiled=True)
    returned = lax.all_to_all(back_sub, 'ep', 3, 0, tiled=True)
    picked = jnp.take(returned.reshape(num_exp * cap_slots, model_dim), slot_of, axis=0).reshape(tok_count, top_k, model_dim)
    moe_sum = jnp.sum(gate_w[:, :, None] * picked.astype(jnp.float32), axis=1)
    out_tok = (flat_tok.astype(jnp.float32) + moe_sum).astype(jnp.bfloat16)
    return out_tok.reshape(seq_count, seq_len, model_dim)


def solution(mesh):
    ep_size = mesh.shape['ep']
    sub_size = mesh.shape['sub']
    tok_spec = P(('dp', 'ep', 'sub'), None, None)
    route_spec = P(None, ('dp', 'ep', 'sub'), None)
    exp_spec = P(('ep', 'sub'), None, None)

    def device_body(input_a, input_b, route_idx, route_gate, attn_norm, w_query, w_key, w_value, w_out, moe_norm, w_gate, w_up, w_down):
        out_a = micro_step(input_a, route_idx[0], route_gate[0], attn_norm, w_query, w_key, w_value, w_out, moe_norm, w_gate, w_up, w_down, ep_size, sub_size)
        out_b = micro_step(input_b, route_idx[1], route_gate[1], attn_norm, w_query, w_key, w_value, w_out, moe_norm, w_gate, w_up, w_down, ep_size, sub_size)
        return out_a, out_b

    return jax.shard_map(device_body, mesh=mesh, in_specs=(tok_spec, tok_spec, route_spec, route_spec, P(), P(), P(), P(), P(), P(), exp_spec, exp_spec, exp_spec), out_specs=(tok_spec, tok_spec), check_vma=False)
```

profile of v0, /device:TPU:0, one launch (start us, length us, event | category | flops | bytes accessed | tf_op | source)
XLA Modules:
  0.0 1932.5 jit_solution(11534534686616132322)
XLA Ops:
  45.1 22.5 %gather_fusion.1 = s32[2048]{0:T(1024)S(1)} fusion(s32[2048]{0:T(1024)S(1)} %reshape_squeeze.7, s32[2048]{0:T(1024)S(1)} %get-tuple-element.137), kind=kCustom, calls=%fused_computation.5 | custom fusion | bytes 24576 | tf_op jit(solution)/shard_map/gather | solution.py:35
  73.4 36.3 %subtract_add_fusion = (s32[2048]{0:T(1024)}, s32[2048]{0:T(1024)S(1)}) fusion(s32[2048]{0:T(1024)S(1)} %gather_fusion.1, pred[2048]{0:T(1024)(128)(4,1)S(1)} %get-tuple-element.64, pred[2048]{0:T(1024)(128)(4,1)S(1)} %get-tuple-element.63, pred[2048]{0:T(1024)(128)(4,1)S(1)} %get-tuple-element.62, pred[2048]{0:T(1024)(128)(4,1)S(1)} %get-tuple-element.61, ...), kind=kLoop, calls=%fused_computation.255 | loop fusion | flops 122880 | bytes 149732 | tf_op jit(solution)/shard_map/add | solution.py:39
  164.2 16.0 gather_fusion.4
  239.2 35.9 %subtract_add_fusion.1 = (s32[2048]{0:T(1024)}, s32[2048]{0:T(1024)S(1)}) fusion(s32[2048]{0:T(1024)S(1)} %gather_fusion, pred[2048]{0:T(1024)(128)(4,1)S(1)} %get-tuple-element.121, pred[2048]{0:T(1024)(128)(4,1)S(1)} %get-tuple-element.120, pred[2048]{0:T(1024)(128)(4,1)S(1)} %get-tuple-element.119, pred[2048]{0:T(1024)(128)(4,1)S(1)} %get-tuple-element.118, ...), kind=kLoop, calls=%fused_computation.258 | loop fusion | flops 122880 | bytes 149732 | tf_op jit(solution)/shard_map/add | solution.py:39
  310.0 26.0 %all-to-all-done.4 = bf16[4,4,4,48,2048]{4,3,2,1,0:T(8,128)(2,1)} async-done(((bf16[4,4,4,48,2048]{4,3,2,1,0:T(8,128)(2,1)}), bf16[4,4,4,48,2048]{4,3,2,1,0:T(8,128)(2,1)}, u32[]{:S(2)}, u32[]{:S(2)}) %all-to-all-start.4) | async-done | bytes 12582944 | tf_op jit(solution)/shard_map/all_to_all | solution.py:64
  353.2 127.0 %all-to-all-done = bf16[4,4,4,48,2048]{4,3,2,1,0:T(8,128)(2,1)} async-done(((bf16[4,4,4,48,2048]{4,3,2,1,0:T(8,128)(2,1)}), bf16[4,4,4,48,2048]{4,3,2,1,0:T(8,128)(2,1)}, u32[]{:S(2)}, u32[]{:S(2)}) %all-to-all-start) | async-done | bytes 12582944 | tf_op jit(solution)/shard_map/all_to_all | solution.py:64
  497.2 262.7 %all-to-all-done.5 = bf16[1,4,4,192,2048]{4,3,2,0,1:T(8,128)(2,1)} async-done(((bf16[1,4,4,192,2048]{4,3,2,0,1:T(8,128)(2,1)}), bf16[1,4,4,192,2048]{4,3,2,0,1:T(8,128)(2,1)}, u32[]{:S(2)}, u32[]{:S(2)}) %all-to-all-start.5) | async-done | bytes 12582944 | tf_op jit(solution)/shard_map/all_to_all | solution.py:65
  772.8 19.4 %fusion.124 = f32[4,768,1024]{2,1,0:T(8,128)} fusion(bf16[4,768,2048]{2,1,0:T(8,128)(2,1)S(1)} %bitcast.290, bf16[4,2048,1024]{2,1,0:T(8,128)(2,1)} %param.27), kind=kOutput, calls=%fused_computation.305 | convolution fusion | flops 12884901888 | bytes 41943040 | tf_op jit(solution)/shard_map/end,edf->enf/dot_general | solution.py:46
  792.2 19.4 %fusion.125 = f32[4,768,1024]{2,1,0:T(8,128)} fusion(bf16[4,768,2048]{2,1,0:T(8,128)(2,1)S(1)} %bitcast.291, bf16[4,2048,1024]{2,1,0:T(8,128)(2,1)} %param.28), kind=kOutput, calls=%fused_computation.306 | convolution fusion | flops 12884901888 | bytes 41943040 | tf_op jit(solution)/shard_map/end,edf->enf/dot_general | solution.py:47
  811.5 24.9 %convert_bitcast_fusion = bf16[1,1,4,768,2048]{4,3,2,1,0:T(8,128)(2,1)} fusion(bf16[4,1024,2048]{2,1,0:T(8,128)(2,1)} %param.29, f32[4,768,1024]{2,1,0:T(8,128)} %fusion.125, f32[4,768,1024]{2,1,0:T(8,128)} %fusion.124), kind=kOutput, calls=%fused_computation.20 | convolution fusion | flops 12910067712 | bytes 54525952 | tf_op jit(solution)/shard_map/enf,efd->end/dot_general | solution.py:49
  836.4 17.1 copy.70
  853.6 185.1 %all-to-all-done.1 = bf16[1,4,4,192,2048]{4,3,2,0,1:T(8,128)(2,1)} async-done(((bf16[1,4,4,192,2048]{4,3,2,0,1:T(8,128)(2,1)}), bf16[1,4,4,192,2048]{4,3,2,0,1:T(8,128)(2,1)}, u32[]{:S(2)}, u32[]{:S(2)}) %all-to-all-start.1) | async-done | bytes 12582944 | tf_op jit(solution)/shard_map/all_to_all | solution.py:65
  1051.3 19.4 %fusion.122 = f32[4,768,1024]{2,1,0:T(8,128)} fusion(bf16[4,768,2048]{2,1,0:T(8,128)(2,1)S(1)} %bitcast.292, bf16[4,2048,1024]{2,1,0:T(8,128)(2,1)} %param.27), kind=kOutput, calls=%fused_computation.303 | convolution fusion | flops 12884901888 | bytes 41943040 | tf_op jit(solution)/shard_map/end,edf->enf/dot_general | solution.py:46
  1070.7 19.5 %fusion.123 = f32[4,768,1024]{2,1,0:T(8,128)} fusion(bf16[4,768,2048]{2,1,0:T(8,128)(2,1)S(1)} %bitcast.293, bf16[4,2048,1024]{2,1,0:T(8,128)(2,1)} %param.28), kind=kOutput, calls=%fused_computation.304 | convolution fusion | flops 12884901888 | bytes 41943040 | tf_op jit(solution)/shard_map/end,edf->enf/dot_general | solution.py:47
  1090.2 25.2 %convert_bitcast_fusion.1 = bf16[1,1,4,768,2048]{4,3,2,1,0:T(8,128)(2,1)} fusion(bf16[4,1024,2048]{2,1,0:T(8,128)(2,1)} %param.29, f32[4,768,1024]{2,1,0:T(8,128)} %fusion.123, f32[4,768,1024]{2,1,0:T(8,128)} %fusion.122), kind=kOutput, calls=%fused_computation.22 | convolution fusion | flops 12910067712 | bytes 54525952 | tf_op jit(solution)/shard_map/enf,efd->end/dot_general | solution.py:49
  1115.3 17.2 copy.55
  1132.5 184.8 %all-to-all-done.6 = bf16[1,1,4,768,2048]{4,2,1,0,3:T(4,128)(2,1)} async-done(((bf16[1,1,4,768,2048]{4,2,1,0,3:T(4,128)(2,1)}), bf16[1,1,4,768,2048]{4,2,1,0,3:T(4,128)(2,1)}, u32[]{:S(2)}, u32[]{:S(2)}) %all-to-all-start.6) | async-done | bytes 12582944 | tf_op jit(solution)/shard_map/all_to_all | solution.py:67
  1323.6 16.4 copy.109
  1340.0 255.8 %all-to-all-done.2 = bf16[1,1,4,768,2048]{4,2,1,0,3:T(4,128)(2,1)} async-done(((bf16[1,1,4,768,2048]{4,2,1,0,3:T(4,128)(2,1)}), bf16[1,1,4,768,2048]{4,2,1,0,3:T(4,128)(2,1)}, u32[]{:S(2)}, u32[]{:S(2)}) %all-to-all-start.2) | async-done | bytes 12582944 | tf_op jit(solution)/shard_map/all_to_all | solution.py:67
  1602.2 16.4 copy.110
  1618.6 121.4 %all-to-all-done.7 = bf16[1,4,4,192,2048]{4,1,2,0,3:T(4,128)(2,1)} async-done(((bf16[1,4,4,192,2048]{4,1,2,0,3:T(4,128)(2,1)}), bf16[1,4,4,192,2048]{4,1,2,0,3:T(4,128)(2,1)}, u32[]{:S(2)}, u32[]{:S(2)}) %all-to-all-start.7) | async-done | bytes 12582944 | tf_op jit(solution)/shard_map/all_to_all | solution.py:68
  1777.9 22.5 %gather_fusion.5 = bf16[2048,2048]{1,0:T(8,128)(2,1)} fusion(bf16[3072,2048]{1,0:T(8,128)(2,1)} %bitcast.282, s32[2048]{0:T(1024)S(1)} %fusion.85), kind=kCustom, calls=%fused_computation.3.clone | custom fusion | bytes 16785408 | tf_op jit(solution)/shard_map/jit(_take)/gather | solution.py:69
  1811.5 72.7 %all-to-all-done.3 = bf16[1,4,4,192,2048]{4,1,2,0,3:T(4,128)(2,1)} async-done(((bf16[1,4,4,192,2048]{4,1,2,0,3:T(4,128)(2,1)}), bf16[1,4,4,192,2048]{4,1,2,0,3:T(4,128)(2,1)}, u32[]{:S(2)}, u32[]{:S(2)}) %all-to-all-start.3) | async-done | bytes 12582944 | tf_op jit(solution)/shard_map/all_to_all | solution.py:68
  1898.8 22.5 %gather_fusion.3 = bf16[2048,2048]{1,0:T(8,128)(2,1)} fusion(bf16[3072,2048]{1,0:T(8,128)(2,1)} %bitcast.283, s32[2048]{0:T(1024)S(1)} %fusion.84), kind=kCustom, calls=%fused_computation.1.clone | custom fusion | bytes 16785408 | tf_op jit(solution)/shard_map/jit(_take)/gather | solution.py:69
  (124 shorter events, 345.2 us)
Async XLA Ops:
  19.5 9.0 slice-start.2
  21.2 7.3 copy-start.3
  21.2 7.3 slice-start.3
  21.2 7.3 copy-start.7
  21.2 11.1 slice-start
  28.5 3.5 copy-start.4
  28.5 3.8 slice-start.1
  134.9 7.1 copy-start.8
  134.9 10.2 copy-start.9
  153.5 8.5 copy-start.6
  162.1 18.2 copy-start
  191.2 144.8 %all-to-all-start.4 = ((bf16[4,4,4,48,2048]{4,3,2,1,0:T(8,128)(2,1)}), bf16[4,4,4,48,2048]{4,3,2,1,0:T(8,128)(2,1)}, u32[]{:S(2)}, u32[]{:S(2)}) async-start(bf16[4,4,4,48,2048]{4,3,2,1,0:T(8,128)(2,1)} %bitcast.284), calls=%async_computation.4 | async-start | bytes 25165824 | tf_op jit(solution)/shard_map/all_to_all | solution.py:64
  336.0 144.1 %all-to-all-start = ((bf16[4,4,4,48,2048]{4,3,2,1,0:T(8,128)(2,1)}), bf16[4,4,4,48,2048]{4,3,2,1,0:T(8,128)(2,1)}, u32[]{:S(2)}, u32[]{:S(2)}) async-start(bf16[4,4,4,48,2048]{4,3,2,1,0:T(8,128)(2,1)} %bitcast.287), calls=%async_computation | async-start | bytes 25165824 | tf_op jit(solution)/shard_map/all_to_all | solution.py:64
  480.1 279.8 %all-to-all-start.5 = ((bf16[1,4,4,192,2048]{4,3,2,0,1:T(8,128)(2,1)}), bf16[1,4,4,192,2048]{4,3,2,0,1:T(8,128)(2,1)}, u32[]{:S(2)}, u32[]{:S(2)}) async-start(bf16[1,4,4,192,2048]{4,3,2,0,1:T(8,128)(2,1)} %bitcast.288), calls=%async_computation.5 | async-start | bytes 25165824 | tf_op jit(solution)/shard_map/all_to_all | solution.py:65
  759.9 278.8 %all-to-all-start.1 = ((bf16[1,4,4,192,2048]{4,3,2,0,1:T(8,128)(2,1)}), bf16[1,4,4,192,2048]{4,3,2,0,1:T(8,128)(2,1)}, u32[]{:S(2)}, u32[]{:S(2)}) async-start(bf16[1,4,4,192,2048]{4,3,2,0,1:T(8,128)(2,1)} %bitcast.286), calls=%async_computation.1 | async-start | bytes 25165824 | tf_op jit(solution)/shard_map/all_to_all | solution.py:65
  1038.7 278.5 %all-to-all-start.6 = ((bf16[1,1,4,768,2048]{4,2,1,0,3:T(4,128)(2,1)}), bf16[1,1,4,768,2048]{4,2,1,0,3:T(4,128)(2,1)}, u32[]{:S(2)}, u32[]{:S(2)}) async-start(bf16[1,1,4,768,2048]{4,2,1,0,3:T(4,128)(2,1)} %copy.70), calls=%async_computation.6 | async-start | bytes 25165824 | tf_op jit(solution)/shard_map/all_to_all | solution.py:67
  1317.3 278.5 %all-to-all-start.2 = ((bf16[1,1,4,768,2048]{4,2,1,0,3:T(4,128)(2,1)}), bf16[1,1,4,768,2048]{4,2,1,0,3:T(4,128)(2,1)}, u32[]{:S(2)}, u32[]{:S(2)}) async-start(bf16[1,1,4,768,2048]{4,2,1,0,3:T(4,128)(2,1)} %copy.55), calls=%async_computation.2 | async-start | bytes 25165824 | tf_op jit(solution)/shard_map/all_to_all | solution.py:67
  1595.8 144.2 %all-to-all-start.7 = ((bf16[1,4,4,192,2048]{4,1,2,0,3:T(4,128)(2,1)}), bf16[1,4,4,192,2048]{4,1,2,0,3:T(4,128)(2,1)}, u32[]{:S(2)}, u32[]{:S(2)}) async-start(bf16[1,4,4,192,2048]{4,1,2,0,3:T(4,128)(2,1)} %bitcast.289), calls=%async_computation.7 | async-start | bytes 25165824 | tf_op jit(solution)/shard_map/all_to_all | solution.py:68
  1740.0 6.5 copy-start.5
  1740.0 144.2 %all-to-all-start.3 = ((bf16[1,4,4,192,2048]{4,1,2,0,3:T(4,128)(2,1)}), bf16[1,4,4,192,2048]{4,1,2,0,3:T(4,128)(2,1)}, u32[]{:S(2)}, u32[]{:S(2)}) async-start(bf16[1,4,4,192,2048]{4,1,2,0,3:T(4,128)(2,1)} %bitcast.285), calls=%async_computation.3 | async-start | bytes 25165824 | tf_op jit(solution)/shard_map/all_to_all | solution.py:68
  1800.4 9.8 copy-start.2
  1921.3 9.8 copy-start.1
where the time goes:
time: 1940 us; the launch traced here: 1930 us
  waiting for transfers between devices  1240 us (64%)
  local copies, waits for them, and re-layouts  281 us (14%)
  other arithmetic  184 us (9%)
  matrix products  179 us (9%)
  starting transfers between devices  51.1 us (3%)
    all_to_all x2, waiting for transfers between devices, micro_step(): arrived = lax.all_to_all(across_ep, 'sub', 1, 3, tiled=True)  448 us
    all_to_all x2, waiting for transfers between devices, micro_step(): lax.all_to_all(expert_out.reshape(1, 1, exp_local, -1, model_dim), 'sub',...  441 us
    all_to_all x2, waiting for transfers between devices, micro_step(): returned = lax.all_to_all(back_sub, 'ep', 3, 0, tiled=True)  194 us
    all_to_all x2, waiting for transfers between devices, micro_step(): across_ep = lax.all_to_all(send_buf, 'ep', 0, 3, tiled=True)  153 us
    add x2, other arithmetic, route_slots(): slot_sorted = sorted_ids * cap_slots + slot_rank  72.1 us
    dot_general x2, matrix products, expert_ffn(): jnp.einsum('enf,efd->end', act_rows, w_down, preferred_element_type=jnp.f...  50.1 us
    gather x2, local copies, waits for them, and re-layouts, micro_step(): jnp.take(returned.reshape(num_exp * cap_slots, model_dim), slot_of, axis=0)  45 us
    dot_general x2, matrix products, expert_ffn(): jnp.einsum('end,edf->enf', disp_rows, w_up, preferred_element_type=jnp.fl...  38.8 us
  transfers between devices with their start and end apart: 8, of which 8 were waited for; matrix products, arithmetic and copies ran while one was open for 21% of the time, Pallas kernels for 0%

commit v1 on v0

v1 whole, which is shorter than its diff:
```python
import functools

import jax
import jax.numpy as jnp
from jax import lax
from jax.experimental import pallas as pl
from jax.experimental.pallas import tpu as pltpu
from jax.sharding import PartitionSpec as P

NORM_EPS = 1e-6
MESH = pl.DeviceIdType.MESH
VMEM_CAP = 60 * 1024 * 1024


def rms_norm(values, norm_gain):
    acc_f32 = values.astype(jnp.float32)
    inv_rms = lax.rsqrt(jnp.mean(acc_f32 * acc_f32, axis=-1, keepdims=True) + NORM_EPS)
    return (acc_f32 * inv_rms * norm_gain).astype(jnp.bfloat16)


def attention_block(tokens, attn_norm, w_query, w_key, w_value, w_out):
    normed = rms_norm(tokens, attn_norm)
    q_heads = jnp.einsum('bsd,dhc->bshc', normed, w_query, preferred_element_type=jnp.float32).astype(jnp.bfloat16)
    k_heads = jnp.einsum('bsd,dhc->bshc', normed, w_key, preferred_element_type=jnp.float32).astype(jnp.bfloat16)
    v_heads = jnp.einsum('bsd,dhc->bshc', normed, w_value, preferred_element_type=jnp.float32).astype(jnp.bfloat16)
    score_scale = w_query.shape[2] ** -0.5
    scores = jnp.einsum('bqhc,bkhc->bhqk', q_heads, k_heads, preferred_element_type=jnp.float32) * score_scale
    seq_len = tokens.shape[1]
    causal = lax.broadcasted_iota(jnp.int32, (seq_len, seq_len), 0) >= lax.broadcasted_iota(jnp.int32, (seq_len, seq_len), 1)
    scores = jnp.where(causal, scores, -jnp.inf)
    prob_bf = jax.nn.softmax(scores, axis=-1).astype(jnp.bfloat16)
    context = jnp.einsum('bhqk,bkhc->bqhc', prob_bf, v_heads, preferred_element_type=jnp.float32).astype(jnp.bfloat16)
    proj_out = jnp.einsum('crid,ide->cre', context, w_out, preferred_element_type=jnp.float32)
    return (tokens.astype(jnp.float32) + proj_out).astype(jnp.bfloat16)


def slot_codes(exp_ids, num_exp, cap_slots):
    hits = exp_ids[:, :, None] == jnp.arange(num_exp, dtype=jnp.int32)[None, None, :]
    chosen = jnp.any(hits, axis=1)
    tok_count = exp_ids.shape[0]
    before = lax.broadcasted_iota(jnp.int32, (tok_count, tok_count), 0) > lax.broadcasted_iota(jnp.int32, (tok_count, tok_count), 1)
    rank = jnp.dot(before.astype(jnp.bfloat16), chosen.astype(jnp.bfloat16), preferred_element_type=jnp.float32)
    rank_of = jnp.sum(jnp.where(hits, rank[:, None, :], 0.0), axis=2)
    return exp_ids.astype(jnp.float32) * cap_slots + rank_of


def greet(sub, sub_size, peers, to_left, to_right):
    barrier = pltpu.get_barrier_semaphore()
    last = sub_size - 1

    def hello(dev):
        pl.semaphore_signal(barrier, inc=1, device_id=dev, device_id_type=MESH)

    for dev in peers:
        hello(dev)
    pl.when(sub > 0)(lambda: hello(to_left))
    pl.when(sub < last)(lambda: hello(to_right))
    pl.semaphore_wait(barrier, len(peers) + (sub + last) // sub_size + (2 * last - sub) // sub_size)


def gather_body(count, sub_size, *refs):
    ins, outs = refs[:count], refs[count:2 * count]
    stage = refs[2 * count:3 * count]
    recv, right_s, left_s, far_s, core_s, loc = refs[3 * count:]
    ep, sub = lax.axis_index('ep'), lax.axis_index('sub')
    ep_far = lax.rem(ep + 2, 4)
    ep_core = ep + 1 - 2 * lax.rem(ep, 2)
    ep_diag = lax.rem(ep_core + 2, 4)
    last = sub_size - 1
    to_right, to_left = {'ep': ep, 'sub': sub + 1}, {'ep': ep, 'sub': sub - 1}
    to_far, to_core = {'ep': ep_far, 'sub': sub}, {'ep': ep_core, 'sub': sub}
    greet(sub, sub_size, [to_far, to_core], to_left, to_right)

    def copies(src, blk, sem, slot, dev):
        return [pltpu.make_async_remote_copy(src_ref=src(a), dst_ref=outs[a].at[blk], send_sem=sem.at[a, slot], recv_sem=recv.at[a, blk], device_id=dev, device_id_type=MESH) for a in range(count)]

    def start(*args):
        for cp in copies(*args):
            cp.start()

    def landed(blk):
        for cp in copies(lambda a: outs[a].at[blk], blk, far_s, 0, to_far):
            cp.wait_recv()

    def sent(sem, slot, dev):
        for cp in copies(lambda a: ins[a], 0, sem, slot, dev):
            cp.wait_send()

    own = lambda a: ins[a]
    me = ep * sub_size + sub
    pl.when(sub < last)(lambda: start(own, me, right_s, sub, to_right))
    pl.when(sub > 0)(lambda: start(own, me, left_s, sub, to_left))
    start(own, me, far_s, sub, to_far)
    start(own, me, core_s, sub, to_core)
    for a in range(count):
        cp = pltpu.make_async_copy(ins[a], stage[a], loc.at[a])
        cp.start()
        cp.wait()
    for a in range(count):
        pltpu.make_async_copy(stage[a], outs[a].at[me], loc.at[a]).start()

    def from_far(src_sub):
        blk = ep_far * sub_size + src_sub
        landed(blk)
        start(lambda a: outs[a].at[blk], blk, core_s, sub_size + src_sub, to_core)

    def from_line(src_sub, sem, cond, dev):
        blk = ep * sub_size + src_sub
        src = lambda a: outs[a].at[blk]
        landed(blk)
        pl.when(cond)(lambda: start(src, blk, sem, src_sub, dev))
        start(src, blk, far_s, src_sub, to_far)
        start(src, blk, core_s, src_sub, to_core)

    for dist in range(1, sub_size):
        pl.when(sub - dist >= 0)(lambda: from_line(sub - dist, right_s, sub < last, to_right))
        pl.when(sub + dist <= last)(lambda: from_line(sub + dist, left_s, sub > 0, to_left))
        if dist == 1:
            from_far(sub)
        else:
            pl.when(sub - dist + 1 >= 0)(lambda: from_far(sub - dist + 1))
            pl.when(sub + dist - 1 <= last)(lambda: from_far(sub + dist - 1))
    pl.when(sub - last >= 0)(lambda: from_far(sub - last))
    pl.when(sub + last <= last)(lambda: from_far(sub + last))

    for src_sub in range(sub_size):
        landed(ep_core * sub_size + src_sub)
        landed(ep_diag * sub_size + src_sub)
    for src_sub in range(sub_size):
        sent(far_s, src_sub, to_far)
        sent(core_s, src_sub, to_core)
        sent(core_s, sub_size + src_sub, to_core)
        pl.when((sub >= src_sub) & (sub < last))(lambda: sent(right_s, src_sub, to_right))
        pl.when((sub <= src_sub) & (sub > 0))(lambda: sent(left_s, src_sub, to_left))
    for a in range(count):
        pltpu.make_async_copy(stage[a], outs[a].at[me], loc.at[a]).wait()


def gather_tokens(arrays, num_dev, sub_size, collective_id):
    count = len(arrays)
    sems = lambda n: pltpu.SemaphoreType.DMA((count, n))
    return pl.pallas_call(
        functools.partial(gather_body, count, sub_size),
        out_shape=[jax.ShapeDtypeStruct((num_dev,) + a.shape, a.dtype) for a in arrays],
        in_specs=[pl.BlockSpec(memory_space=pl.ANY)] * count,
        out_specs=[pl.BlockSpec(memory_space=pl.ANY)] * count,
        scratch_shapes=[pltpu.VMEM(a.shape, a.dtype) for a in arrays] + [sems(num_dev), sems(sub_size), sems(sub_size), sems(sub_size), sems(2 * sub_size), pltpu.SemaphoreType.DMA((count,))],
        compiler_params=pltpu.CompilerParams(collective_id=collective_id, has_side_effects=True, vmem_limit_bytes=VMEM_CAP),
        name='gather_tokens',
    )(*arrays)


def pick_body(exp_local, cap_slots, base_ref, code_ref, tok_ref, out_ref):
    room = exp_local * cap_slots
    top_k, tok_count = code_ref.shape[1] // 2, code_ref.shape[2]
    want = lax.broadcasted_iota(jnp.int32, (room, tok_count), 0).astype(jnp.float32) + base_ref[0].astype(jnp.float32)
    hit = code_ref[0, 0:1, :] == want
    for j in range(1, top_k):
        hit = hit | (code_ref[0, j:j + 1, :] == want)
    onehot = jnp.where(hit, 1.0, 0.0).astype(jnp.bfloat16)
    picked = jnp.dot(onehot, tok_ref[0], preferred_element_type=jnp.float32).astype(jnp.bfloat16)
    for e in range(exp_local):
        out_ref[e] = picked[e * cap_slots:(e + 1) * cap_slots]


def pick_rows(base, codes, gathered, exp_local, cap_slots):
    num_dev, tok_count, dim = gathered.shape
    return pl.pallas_call(
        functools.partial(pick_body, exp_local, cap_slots),
        grid=(num_dev,),
        out_shape=jax.ShapeDtypeStruct((exp_local, num_dev * cap_slots, dim), jnp.bfloat16),
        in_specs=[
            pl.BlockSpec(memory_space=pltpu.SMEM),
            pl.BlockSpec((1,) + codes.shape[1:], lambda s: (s, 0, 0)),
            pl.BlockSpec((1, tok_count, dim), lambda s: (s, 0, 0)),
        ],
        out_specs=pl.BlockSpec((exp_local, cap_slots, dim), lambda s: (0, s, 0)),
        compiler_params=pltpu.CompilerParams(vmem_limit_bytes=VMEM_CAP),
        name='pick_rows',
    )(base, codes, gathered)


def ffn_body(steps, x_ref, w1_ref, w3_ref, w2_ref, out_ref, act_ref):
    step = pl.program_id(1)

    @pl.when(step < steps)
    def _():
        x = x_ref[0]
        gate_h = jnp.dot(x, w1_ref[0], preferred_element_type=jnp.float32)
        up_h = jnp.dot(x, w3_ref[0], preferred_element_type=jnp.float32)
        act_ref[step] = (jax.nn.silu(gate_h) * up_h).astype(jnp.bfloat16)

    @pl.when(step >= steps)
    def _():
        tile = w2_ref.shape[1] // steps
        acc = jnp.dot(act_ref[0], w2_ref[0, 0:tile, :], preferred_element_type=jnp.float32)
        for k in range(1, steps):
            acc = acc + jnp.dot(act_ref[k], w2_ref[0, k * tile:(k + 1) * tile, :], preferred_element_type=jnp.float32)
        out_ref[...] = acc.astype(jnp.bfloat16).reshape(out_ref.shape)


def expert_ffn(rows, w_gate, w_up, w_down, num_dev, cap_slots):
    exp_local, room, dim = rows.shape
    ff = w_gate.shape[2]
    steps = 4
    ft, nt = ff // steps, dim // steps
    return pl.pallas_call(
        functools.partial(ffn_body, steps),
        grid=(exp_local, 2 * steps),
        out_shape=jax.ShapeDtypeStruct((num_dev, exp_local, cap_slots, dim), jnp.bfloat16),
        in_specs=[
            pl.BlockSpec((1, room, dim), lambda e, s: (e, 0, 0)),
            pl.BlockSpec((1, dim, ft), lambda e, s: (e, 0, jnp.minimum(s, steps - 1))),
            pl.BlockSpec((1, dim, ft), lambda e, s: (e, 0, jnp.minimum(s, steps - 1))),
            pl.BlockSpec((1, ff, nt), lambda e, s: (e, 0, jnp.maximum(s - steps, 0))),
        ],
        out_specs=pl.BlockSpec((num_dev, 1, cap_slots, nt), lambda e, s: (0, e, 0, jnp.maximum(s - steps, 0))),
        scratch_shapes=[pltpu.VMEM((steps, room, ft), jnp.bfloat16)],
        compiler_params=pltpu.CompilerParams(vmem_limit_bytes=VMEM_CAP),
        name='expert_ffn',
    )(rows, w_gate, w_up, w_down)


PARTS = 2


def combine_body(sub_size, e_ref, col_ref, gate_ref, hid_ref, out_ref, slots, sums, from_left, from_right, mix, a_recv, a_send, a_loc, l_recv, r_recv, z_send):
    ep, sub = lax.axis_index('ep'), lax.axis_index('sub')
    ep_far = lax.rem(ep + 2, 4)
    ep_core = ep + 1 - 2 * lax.rem(ep, 2)
    ep_diag = lax.rem(ep_core + 2, 4)
    last = sub_size - 1
    room, dim = e_ref.shape[1], e_ref.shape[2]
    tok_count, top_k = col_ref.shape[1], col_ref.shape[2]
    width = dim // PARTS
    to_right, to_left = {'ep': ep, 'sub': sub + 1}, {'ep': ep, 'sub': sub - 1}
    peers = [ep_far, ep_diag, ep_core]
    greet(sub, sub_size, [{'ep': p, 'sub': sub} for p in peers], to_left, to_right)

    side = sub // 2
    near = sub + side * (3 - 2 * sub)
    order = [a + side * (3 - 2 * a) for a in (3, 2 - 2 * near, 1 + near, near)]

    def part(h):
        return pl.ds(h * width, width)

    def slot_copy(dst, k, h):
        peer = peers[k]
        return pltpu.make_async_remote_copy(
            src_ref=e_ref.at[peer * sub_size + dst, :, part(h)], dst_ref=slots.at[dst, pl.ds(pl.multiple_of(ep * room, room), room), part(h)],
            send_sem=a_send.at[dst, k, h], recv_sem=a_recv.at[dst, ep, h], device_id={'ep': peer, 'sub': sub}, device_id_type=MESH)

    def slot_landed(dst, k, h):
        peer = peers[k]
        pltpu.make_async_remote_copy(
            src_ref=e_ref.at[peer * sub_size + dst, :, part(h)], dst_ref=slots.at[dst, pl.ds(pl.multiple_of(peer * room, room), room), part(h)],
            send_sem=a_send.at[dst, k, h], recv_sem=a_recv.at[dst, peer, h], device_id={'ep': peer, 'sub': sub}, device_id_type=MESH).wait_recv()

    def own_copy(dst):
        return pltpu.make_async_copy(e_ref.at[ep * sub_size + dst], slots.at[dst, pl.ds(pl.multiple_of(ep * room, room), room), :], a_loc.at[dst])

    def line_copy(dst, h, right):
        inbox, sem, dev = (from_left, l_recv, to_right) if right else (from_right, r_recv, to_left)
        return pltpu.make_async_remote_copy(
            src_ref=sums.at[dst, :, part(h)], dst_ref=inbox.at[dst, :, part(h)],
            send_sem=z_send.at[dst, h], recv_sem=sem.at[dst, h], device_id=dev, device_id_type=MESH)

    for dst in order:
        for h in range(PARTS):
            for k in range(3):
                slot_copy(dst, k, h).start()
        own_copy(dst).start()

    for i, dst in enumerate(order):
        cols = lax.broadcasted_iota(jnp.int32, (tok_count, 4 * room), 1)
        mat = jnp.zeros((tok_count, 4 * room), jnp.float32)
        for j in range(top_k):
            mat = jnp.where(col_ref[dst, :, j:j + 1] == cols, gate_ref[dst, :, j:j + 1], mat)
        for s in range(3):
            piece = mat.astype(jnp.bfloat16)
            mix[s * tok_count:(s + 1) * tok_count, :] = piece
            mat = mat - piece.astype(jnp.float32)
        own_copy(dst).wait()
        for h in range(PARTS):
            for k in range(3):
                slot_landed(dst, k, h)
            tile = 256
            for c in range(width // tile):
                cs = pl.ds(h * width + c * tile, tile)
                prod = jnp.dot(mix[...], slots[dst, :, cs], preferred_element_type=jnp.float32)
                sums[dst, :, cs] = prod[0:tok_count] + (prod[tok_count:2 * tok_count] + prod[2 * tok_count:])

            def add(inbox, sem, right):
                line_copy(dst, h, right).wait_recv()
                sums[dst, :, part(h)] = sums[dst, :, part(h)] + inbox[dst, :, part(h)]

            if i < last:
                pl.when((dst > sub) & (sub > 0))(lambda: add(from_left, l_recv, True))
                pl.when((dst < sub) & (sub < last))(lambda: add(from_right, r_recv, False))
                pl.when(dst > sub)(lambda: line_copy(dst, h, True).start())
                pl.when(dst < sub)(lambda: line_copy(dst, h, False).start())
            else:
                pl.when(sub > 0)(lambda: add(from_left, l_recv, True))
                pl.when(sub < last)(lambda: add(from_right, r_recv, False))
                out_ref[:, part(h)] = (hid_ref[:, part(h)].astype(jnp.float32) + sums[dst, :, part(h)]).astype(jnp.bfloat16)

    for i, dst in enumerate(order):
        for h in range(PARTS):
            for k in range(3):
                slot_copy(dst, k, h).wait_send()
            if i < last:
                pl.when(dst > sub)(lambda: line_copy(dst, h, True).wait_send())
                pl.when(dst < sub)(lambda: line_copy(dst, h, False).wait_send())


def combine_rows(expert_rows, cols, gates, hidden, sub_size, collective_id):
    num_dev, room, dim = expert_rows.shape
    tok_count = hidden.shape[0]
    dma = lambda *s: pltpu.SemaphoreType.DMA(s)
    vmem = pl.BlockSpec(memory_space=pltpu.VMEM)
    return pl.pallas_call(
        functools.partial(combine_body, sub_size),
        out_shape=jax.ShapeDtypeStruct((tok_count, dim), jnp.bfloat16),
        in_specs=[pl.BlockSpec(memory_space=pl.ANY), vmem, vmem, vmem],
        out_specs=vmem,
        scratch_shapes=[
            pltpu.VMEM((sub_size, 4 * room, dim), jnp.bfloat16),
            pltpu.VMEM((sub_size, tok_count, dim), jnp.float32),
            pltpu.VMEM((sub_size, tok_count, dim), jnp.float32),
            pltpu.VMEM((sub_size, tok_count, dim), jnp.float32),
            pltpu.VMEM((3 * tok_count, 4 * room), jnp.bfloat16),
            dma(sub_size, 4, PARTS), dma(sub_size, 3, PARTS), dma(sub_size,),
            dma(sub_size, PARTS), dma(sub_size, PARTS), dma(sub_size, PARTS),
        ],
        compiler_params=pltpu.CompilerParams(collective_id=collective_id, has_side_effects=True, vmem_limit_bytes=VMEM_CAP),
        name='combine_rows',
    )(expert_rows, cols, gates, hidden)


def solution(mesh):
    ep_size = mesh.shape['ep']
    sub_size = mesh.shape['sub']
    num_dev = ep_size * sub_size
    tok_spec = P(('dp', 'ep', 'sub'), None, None)
    route_spec = P(None, ('dp', 'ep', 'sub'), None)
    exp_spec = P(('ep', 'sub'), None, None)

    def device_body(input_a, input_b, route_idx, route_gate, attn_norm, w_query, w_key, w_value, w_out, moe_norm, w_gate, w_up, w_down):
        exp_local = w_gate.shape[0]
        num_exp = exp_local * num_dev
        tok_count, top_k = route_idx.shape[1:]
        dim = input_a.shape[2]
        cap_slots = 3 * top_k * tok_count // (2 * num_exp)
        room = exp_local * cap_slots
        ep, sub = lax.axis_index('ep'), lax.axis_index('sub')

        meta = jnp.concatenate([jnp.stack([slot_codes(route_idx[m], num_exp, cap_slots) for m in range(2)]), route_gate], axis=2)
        meta = meta.transpose(0, 2, 1)
        hidden = [attention_block(x, attn_norm, w_query, w_key, w_value, w_out).reshape(tok_count, dim) for x in (input_a, input_b)]
        normed = [rms_norm(h, moe_norm) for h in hidden]
        gath_a, metas = gather_tokens([normed[0], meta], num_dev, sub_size, 1)
        gath_b, = gather_tokens([normed[1]], num_dev, sub_size, 2)
        base = ((ep * sub_size + sub) * room).astype(jnp.int32).reshape(1)
        mine = lax.dynamic_slice_in_dim(metas, ep * sub_size, sub_size, axis=0)
        code = mine[:, :, :top_k, :].astype(jnp.int32).transpose(1, 0, 3, 2)
        gates = mine[:, :, top_k:, :].transpose(1, 0, 3, 2)
        dev_of = code // room
        cols = jnp.where(dev_of % sub_size == sub, (dev_of // sub_size) * room + code % room, -1)
        outs = []
        for m, gathered in enumerate((gath_a, gath_b)):
            rows = pick_rows(base, metas[:, m], gathered, exp_local, cap_slots)
            expert_rows = expert_ffn(rows, w_gate, w_up, w_down, num_dev, cap_slots).reshape(num_dev, room, dim)
            outs.append(combine_rows(expert_rows, cols[m], gates[m], hidden[m], sub_size, 3 + m).reshape(1, tok_count, dim))
        return tuple(outs)

    return jax.shard_map(device_body, mesh=mesh, in_specs=(tok_spec, tok_spec, route_spec, route_spec, P(), P(), P(), P(), P(), P(), exp_spec, exp_spec, exp_spec), out_specs=(tok_spec, tok_spec), check_vma=False)
```

time: 1940 us -> 782 us (0.40)
  waiting for transfers between devices: 1240 us -> 0 us
  Pallas kernels: 0 us -> 680 us
  local copies, waits for them, and re-layouts: 281 us -> 11.5 us
  other arithmetic: 184 us -> 22 us
  matrix products: 179 us -> 56.6 us
  starting transfers between devices: 51.1 us -> 0 us
    all_to_all x8 -> x0, waiting for transfers between devices: 1240 us -> none  [the longest x2 448 us: micro_step(): arrived = lax.all_to_all(across_ep, 'sub', 1, 3, tiled=True)]
    pallas_call x0 -> x8, Pallas kernels: none -> 680 us  [the longest x2 319 us: combine_rows(): pl.pallas_call(functools.partial(combine_body, sub_size), out_shape=jax.S...]
    dot_general x6 -> x2, matrix products: 128 us -> 0.34 us  [slot_codes(): jnp.dot(before.astype(jnp.bfloat16), chosen.astype(jnp.bfloat16), preferr...]
    gather x14 -> x0, local copies, waits for them, and re-layouts: 117 us -> none  [the longest x2 45 us: micro_step(): jnp.take(returned.reshape(num_exp * cap_slots, model_dim), slot_of, axis=0)]
    all_to_all x8 -> x0, local copies, waits for them, and re-layouts: 96 us -> none  [the longest x2 32.7 us: micro_step(): lax.all_to_all(expert_out.reshape(1, 1, exp_local, -1, model_dim), 'sub',...]
    add x2 -> x1, other arithmetic: 72.1 us -> 0.01 us  [slot_codes(): return exp_ids.astype(jnp.float32) * cap_slots + rank_of]
    all_to_all x8 -> x0, starting transfers between devices: 51.1 us -> none  [the longest x2 12.9 us: micro_step(): returned = lax.all_to_all(back_sub, 'ep', 3, 0, tiled=True)]
    reshape x2 -> x0, local copies, waits for them, and re-layouts: 34.3 us -> none  [micro_step(): expert_out.reshape(1, 1, exp_local, -1, model_dim)]
  transfers between devices with their start and end apart: 8 -> 0, of which waited for: 8 -> 0; matrix products, arithmetic and copies ran while one was open for 21% -> 0% of each run, Pallas kernels for 0% -> 0%
where the time goes in v1:
time: 782 us; the launch traced here: 772 us
  Pallas kernels  680 us (87%)
  matrix products  56.6 us (7%)
  other arithmetic  22 us (3%)
  local copies, waits for them, and re-layouts  11.5 us (1%)
    pallas_call x2, Pallas kernels, combine_rows(): pl.pallas_call(functools.partial(combine_body, sub_size), out_shape=jax.S...  319 us
    pallas_call x2, Pallas kernels, gather_tokens(): pl.pallas_call(functools.partial(gather_body, count, sub_size), out_shape...  204 us
    pallas_call x2, Pallas kernels, expert_ffn(): pl.pallas_call(functools.partial(ffn_body, steps), grid=(exp_local, 2 * s...  119 us
    pallas_call x2, Pallas kernels, pick_rows(): pl.pallas_call(functools.partial(pick_body, exp_local, cap_slots), grid=(...  38.1 us
    dot_general x2, matrix products, attention_block(): jnp.einsum('bqhc,bkhc->bhqk', q_heads, k_heads, preferred_element_type=jn...  16.7 us
    dot_general x2, matrix products, attention_block(): jnp.einsum('crid,ide->cre', context, w_out, preferred_element_type=jnp.fl...  15.8 us

profile of v1, /device:TPU:0, one launch (start us, length us, event | category | flops | bytes accessed | tf_op | source)
XLA Modules:
  0.0 771.6 jit_solution(6272932797863156897)
XLA Ops:
  0.6 1.7 fusion.29
  2.4 7.2 fusion.45
  9.6 2.4 fusion.63
  12.0 8.3 %fusion.58 = f32[16,256,256]{1,2,0:T(8,128)} fusion(bf16[256,16,128]{2,0,1:T(8,128)(2,1)S(1)} %fusion.63, bf16[2048,16,128]{2,1,0:T(8,128)(2,1)} %param.18, bf16[1,256,2048]{2,1,0:T(8,128)(2,1)S(1)} %copy-done.4, f32[256]{0:T(256)S(1)} %add_rsqrt_fusion.1, f32[2048]{0:T(1024)S(1)} %copy-done.9), kind=kOutput, calls=%fused_computation.72 | convolution fusion | flops 2418540544 | bytes 14689280 | tf_op jit(solution)/shard_map/bqhc,bkhc->bhqk/dot_general | solution.py:27
  20.3 7.0 fusion.95
  27.3 7.9 %fusion.23 = (f32[256]{0:T(256)S(1)}, bf16[256,2048]{1,0:T(8,128)(2,1)S(1)}) fusion(bf16[16,128,2048]{2,1,0:T(8,128)(2,1)} %param.21, bf16[256,16,128]{2,0,1:T(8,128)(2,1)} %fusion.45, f32[16,256,256]{1,2,0:T(8,128)} %get-tuple-element.19, f32[16,256]{1,0:T(8,128)S(1)} %get-tuple-element.18, bf16[1,256,2048]{2,1,0:T(8,128)(2,1)S(1)} %copy-done.4), kind=kOutput, calls=%fused_computation.41 | convolution fusion | flops 2421686016 | bytes 15746048 | tf_op jit(solution)/shard_map/crid,ide->cre/dot_general | solution.py:33
  35.6 7.3 fusion.42
  42.9 6.7 fusion.60
  49.6 8.5 %fusion.52 = f32[16,256,256]{1,2,0:T(8,128)} fusion(bf16[256,16,128]{2,0,1:T(8,128)(2,1)} %fusion.60, bf16[2048,16,128]{2,1,0:T(8,128)(2,1)} %param.18, bf16[1,256,2048]{2,1,0:T(8,128)(2,1)S(1)} %copy-done.5, f32[2048]{0:T(1024)S(1)} %copy-done.9, f32[256]{0:T(256)S(1)} %add_rsqrt_fusion.3), kind=kOutput, calls=%fused_computation.70 | convolution fusion | flops 2418540544 | bytes 14689280 | tf_op jit(solution)/shard_map/bqhc,bkhc->bhqk/dot_general | solution.py:27
  58.1 7.0 fusion.96
  65.1 7.9 %fusion.20 = (f32[256]{0:T(256)S(1)}, bf16[256,2048]{1,0:T(8,128)(2,1)S(1)}) fusion(bf16[16,128,2048]{2,1,0:T(8,128)(2,1)} %param.21, bf16[256,16,128]{2,0,1:T(8,128)(2,1)} %fusion.42, f32[16,256,256]{1,2,0:T(8,128)} %get-tuple-element.23, f32[16,256]{1,0:T(8,128)S(1)} %get-tuple-element.22, bf16[1,256,2048]{2,1,0:T(8,128)(2,1)S(1)} %copy-done.5), kind=kOutput, calls=%fused_computation.38 | convolution fusion | flops 2421686016 | bytes 15746048 | tf_op jit(solution)/shard_map/crid,ide->cre/dot_general | solution.py:33
  73.0 1.9 fusion.25
  76.2 104.5 %gather_tokens.2 = (bf16[16,256,2048]{2,1,0:T(8,128)(2,1)}, f32[16,2,16,256]{3,2,1,0:T(8,128)}) custom-call(bf16[256,2048]{1,0:T(8,128)(2,1)} %get-tuple-element.17.refs_0_, f32[2,16,256]{2,1,0:T(8,128)} %maximum_bitcast_fusion.refs_1_), custom_call_target="tpu_custom_call" | custom-call | tf_op jit(solution)/shard_map/gather_tokens/pallas_call | solution.py:142
  180.7 1.9 slice_bitcast_fusion.4
  182.6 19.0 %pick_rows.2.x_ref = bf16[4,768,2048]{2,1,0:T(8,128)(2,1)} custom-call(s32[1]{0:T(128)} %bitcast.base_ref, f32[16,16,256]{2,1,0:T(8,128)} %get-tuple-element.11.code_ref, bf16[16,256,2048]{2,1,0:T(8,128)(2,1)} %get-tuple-element.5.tok_ref), custom_call_target="tpu_custom_call" | custom-call | tf_op jit(solution)/shard_map/pick_rows/pallas_call | solution.py:168
  201.6 59.4 %expert_ffn.2 = bf16[16,4,48,2048]{3,2,1,0:T(8,128)(2,1)} custom-call(bf16[4,768,2048]{2,1,0:T(8,128)(2,1)} %pick_rows.2.x_ref, bf16[4,2048,1024]{2,1,0:T(8,128)(2,1)} %w1_ref.3, bf16[4,2048,1024]{2,1,0:T(8,128)(2,1)} %w3_ref.3, bf16[4,1024,2048]{2,1,0:T(8,128)(2,1)} %w2_ref.3), custom_call_target="tpu_custom_call" | custom-call | tf_op jit(solution)/shard_map/expert_ffn/pallas_call | solution.py:207
  261.0 2.6 copy.40
  263.6 3.3 fusion.71
  270.6 159.6 %combine_rows.2 = bf16[256,2048]{1,0:T(8,128)(2,1)} custom-call(bf16[16,192,2048]{2,1,0:T(8,128)(2,1)} %bitcast.115, s32[4,256,8]{2,1,0:T(8,128)} %get-tuple-element.9.col_ref, f32[4,256,8]{2,1,0:T(8,128)} %get-tuple-element.7.gate_ref, bf16[256,2048]{1,0:T(8,128)(2,1)} %copy-done.2), custom_call_target="tpu_custom_call" | custom-call | tf_op jit(solution)/shard_map/combine_rows/pallas_call | solution.py:321
  430.1 99.4 %gather_tokens.3.tok_ref = bf16[16,256,2048]{2,1,0:T(8,128)(2,1)} custom-call(bf16[256,2048]{1,0:T(8,128)(2,1)} %get-tuple-element.16.refs_0_), custom_call_target="tpu_custom_call" | custom-call | tf_op jit(solution)/shard_map/gather_tokens/pallas_call | solution.py:142
  529.5 19.0 %pick_rows.3.x_ref = bf16[4,768,2048]{2,1,0:T(8,128)(2,1)} custom-call(s32[1]{0:T(128)} %bitcast.base_ref, f32[16,16,256]{2,1,0:T(8,128)} %get-tuple-element.10.code_ref, bf16[16,256,2048]{2,1,0:T(8,128)(2,1)} %gather_tokens.3.tok_ref), custom_call_target="tpu_custom_call" | custom-call | tf_op jit(solution)/shard_map/pick_rows/pallas_call | solution.py:168
  548.6 59.4 %expert_ffn.3 = bf16[16,4,48,2048]{3,2,1,0:T(8,128)(2,1)} custom-call(bf16[4,768,2048]{2,1,0:T(8,128)(2,1)} %pick_rows.3.x_ref, bf16[4,2048,1024]{2,1,0:T(8,128)(2,1)} %w1_ref.3, bf16[4,2048,1024]{2,1,0:T(8,128)(2,1)} %w3_ref.3, bf16[4,1024,2048]{2,1,0:T(8,128)(2,1)} %w2_ref.3), custom_call_target="tpu_custom_call" | custom-call | tf_op jit(solution)/shard_map/expert_ffn/pallas_call | solution.py:207
  607.9 159.9 %combine_rows.3 = bf16[256,2048]{1,0:T(8,128)(2,1)} custom-call(bf16[16,192,2048]{2,1,0:T(8,128)(2,1)} %bitcast.116, s32[4,256,8]{2,1,0:T(8,128)} %get-tuple-element.8.col_ref, f32[4,256,8]{2,1,0:T(8,128)} %get-tuple-element.6.gate_ref, bf16[256,2048]{1,0:T(8,128)(2,1)} %copy-done.1), custom_call_target="tpu_custom_call" | custom-call | tf_op jit(solution)/shard_map/combine_rows/pallas_call | solution.py:321
  768.8 2.3 copy.87
  (42 shorter events, 6.3 us)
Async XLA Ops:
  0.6 9.0 %slice-start = ((s8[8388608]{0:T(1024)(128)(4,1)}), s8[4194304]{0:T(1024)(128)(4,1)S(1)}, s32[]{:S(2)}) async-start(s8[8388608]{0:T(1024)(128)(4,1)} %bitcast.119), calls=%async_computation | async-start | bytes 8388608
  2.3 7.3 copy-start.4
  2.3 7.3 slice-start.1
  2.3 7.3 copy-start.9
  27.3 7.9 %copy-start.5 = (bf16[1,256,2048]{2,1,0:T(8,128)(2,1)S(1)}, bf16[1,256,2048]{2,1,0:T(8,128)(2,1)}, u32[]{:S(2)}) copy-start(bf16[1,256,2048]{2,1,0:T(8,128)(2,1)} %param.13) | copy-start | bytes 3145732
  35.3 37.7 %copy-start.1 = (bf16[256,2048]{1,0:T(8,128)(2,1)}, bf16[256,2048]{1,0:T(8,128)(2,1)S(1)}, u32[]{:S(2)}) copy-start(bf16[256,2048]{1,0:T(8,128)(2,1)S(1)} %get-tuple-element.21.hid_ref) | copy-start | bytes 3145732
  65.1 7.9 %copy-start.8 = (f32[2048]{0:T(1024)S(1)}, f32[2048]{0:T(1024)}, u32[]{:S(2)}) copy-start(f32[2048]{0:T(1024)} %param.22) | copy-start | bytes 24580
  72.9 128.6 %copy-start.2 = (bf16[256,2048]{1,0:T(8,128)(2,1)}, bf16[256,2048]{1,0:T(8,128)(2,1)S(1)}, u32[]{:S(2)}) copy-start(bf16[256,2048]{1,0:T(8,128)(2,1)S(1)} %get-tuple-element.25.hid_ref) | copy-start | bytes 3145732
  73.0 1.9 copy-start.6
  73.0 2.6 copy-start.7
  201.6 59.4 %copy-start.3 = (f32[16,2,16,256]{3,2,1,0:T(8,128)S(1)}, f32[16,2,16,256]{3,2,1,0:T(8,128)}, u32[]{:S(2)}) copy-start(f32[16,2,16,256]{3,2,1,0:T(8,128)} %get-tuple-element.4) | copy-start | bytes 1572868
  607.9 159.9 %copy-start = (bf16[256,2048]{1,0:T(8,128)(2,1)S(1)}, bf16[256,2048]{1,0:T(8,128)(2,1)}, u32[]{:S(2)}) copy-start(bf16[256,2048]{1,0:T(8,128)(2,1)} %combine_rows.2) | copy-start | bytes 3145732

commit v2 on v0

v2 whole, which is shorter than its diff:
```python
import functools

import jax
import jax.numpy as jnp
from jax import lax
from jax.experimental import pallas as pl
from jax.experimental.pallas import tpu as pltpu
from jax.sharding import PartitionSpec as P

NORM_EPS = 1e-6
MESH = pl.DeviceIdType.MESH
VMEM_CAP = 60 * 1024 * 1024
ANY = pl.BlockSpec(memory_space=pl.ANY)


def rms_norm(values, norm_gain):
    acc_f32 = values.astype(jnp.float32)
    inv_rms = lax.rsqrt(jnp.mean(acc_f32 * acc_f32, axis=-1, keepdims=True) + NORM_EPS)
    return (acc_f32 * inv_rms * norm_gain).astype(jnp.bfloat16)


def attention_block(tokens, attn_norm, w_query, w_key, w_value, w_out):
    normed = rms_norm(tokens, attn_norm)
    q_heads = jnp.einsum('bsd,dhc->bshc', normed, w_query, preferred_element_type=jnp.float32).astype(jnp.bfloat16)
    k_heads = jnp.einsum('bsd,dhc->bshc', normed, w_key, preferred_element_type=jnp.float32).astype(jnp.bfloat16)
    v_heads = jnp.einsum('bsd,dhc->bshc', normed, w_value, preferred_element_type=jnp.float32).astype(jnp.bfloat16)
    score_scale = w_query.shape[2] ** -0.5
    scores = jnp.einsum('bqhc,bkhc->bhqk', q_heads, k_heads, preferred_element_type=jnp.float32) * score_scale
    seq_len = tokens.shape[1]
    causal = lax.broadcasted_iota(jnp.int32, (seq_len, seq_len), 0) >= lax.broadcasted_iota(jnp.int32, (seq_len, seq_len), 1)
    scores = jnp.where(causal, scores, -jnp.inf)
    prob_bf = jax.nn.softmax(scores, axis=-1).astype(jnp.bfloat16)
    context = jnp.einsum('bhqk,bkhc->bqhc', prob_bf, v_heads, preferred_element_type=jnp.float32).astype(jnp.bfloat16)
    proj_out = jnp.einsum('crid,ide->cre', context, w_out, preferred_element_type=jnp.float32)
    return (tokens.astype(jnp.float32) + proj_out).astype(jnp.bfloat16)


def slot_codes(exp_ids, num_exp, cap_slots):
    hits = exp_ids[:, :, None] == jnp.arange(num_exp, dtype=jnp.int32)[None, None, :]
    chosen = jnp.any(hits, axis=1)
    tok_count = exp_ids.shape[0]
    before = lax.broadcasted_iota(jnp.int32, (tok_count, tok_count), 0) > lax.broadcasted_iota(jnp.int32, (tok_count, tok_count), 1)
    rank = jnp.dot(before.astype(jnp.bfloat16), chosen.astype(jnp.bfloat16), preferred_element_type=jnp.float32)
    rank_of = jnp.sum(jnp.where(hits, rank[:, None, :], 0.0), axis=2)
    return exp_ids.astype(jnp.float32) * cap_slots + rank_of


def greet(sub, sub_size, peers, to_left, to_right):
    barrier = pltpu.get_barrier_semaphore()
    last = sub_size - 1

    def hello(dev):
        pl.semaphore_signal(barrier, inc=1, device_id=dev, device_id_type=MESH)

    for dev in peers:
        hello(dev)
    pl.when(sub > 0)(lambda: hello(to_left))
    pl.when(sub < last)(lambda: hello(to_right))
    pl.semaphore_wait(barrier, len(peers) + (sub + last) // sub_size + (2 * last - sub) // sub_size)


class Gather:
    def __init__(self, sub_size, ins, outs, stage, recv, right_s, left_s, far_s, core_s, loc):
        self.count, self.sub_size = len(ins), sub_size
        self.ins, self.outs, self.stage = ins, outs, stage
        self.recv, self.right_s, self.left_s, self.far_s, self.core_s, self.loc = recv, right_s, left_s, far_s, core_s, loc
        ep, sub = lax.axis_index('ep'), lax.axis_index('sub')
        self.ep, self.sub, self.last = ep, sub, sub_size - 1
        self.ep_far = lax.rem(ep + 2, 4)
        self.ep_core = ep + 1 - 2 * lax.rem(ep, 2)
        self.ep_diag = lax.rem(self.ep_core + 2, 4)
        self.me = ep * sub_size + sub
        self.to_right, self.to_left = {'ep': ep, 'sub': sub + 1}, {'ep': ep, 'sub': sub - 1}
        self.to_far, self.to_core = {'ep': self.ep_far, 'sub': sub}, {'ep': self.ep_core, 'sub': sub}

    def copies(self, src, blk, sem, slot, dev):
        return [pltpu.make_async_remote_copy(src_ref=src(a), dst_ref=self.outs[a].at[blk], send_sem=sem.at[a, slot], recv_sem=self.recv.at[a, blk], device_id=dev, device_id_type=MESH) for a in range(self.count)]

    def start(self, *args):
        for cp in self.copies(*args):
            cp.start()

    def landed(self, blk):
        for cp in self.copies(lambda a: self.outs[a].at[blk], blk, self.far_s, 0, self.to_far):
            cp.wait_recv()

    def sent(self, sem, slot, dev):
        for cp in self.copies(lambda a: self.ins[a], 0, sem, slot, dev):
            cp.wait_send()

    def begin(self):
        own = lambda a: self.ins[a]
        sub, me = self.sub, self.me
        greet(sub, self.sub_size, [self.to_far, self.to_core], self.to_left, self.to_right)
        pl.when(sub < self.last)(lambda: self.start(own, me, self.right_s, sub, self.to_right))
        pl.when(sub > 0)(lambda: self.start(own, me, self.left_s, sub, self.to_left))
        self.start(own, me, self.far_s, sub, self.to_far)
        self.start(own, me, self.core_s, sub, self.to_core)
        for a in range(self.count):
            cp = pltpu.make_async_copy(self.ins[a], self.stage[a], self.loc.at[a])
            cp.start()
            cp.wait()
        for a in range(self.count):
            pltpu.make_async_copy(self.stage[a], self.outs[a].at[me], self.loc.at[a]).start()

    def from_far(self, src_sub):
        blk = self.ep_far * self.sub_size + src_sub
        self.landed(blk)
        self.start(lambda a: self.outs[a].at[blk], blk, self.core_s, self.sub_size + src_sub, self.to_core)

    def from_line(self, src_sub, sem, cond, dev):
        blk = self.ep * self.sub_size + src_sub
        src = lambda a: self.outs[a].at[blk]
        self.landed(blk)
        pl.when(cond)(lambda: self.start(src, blk, sem, src_sub, dev))
        self.start(src, blk, self.far_s, src_sub, self.to_far)
        self.start(src, blk, self.core_s, src_sub, self.to_core)

    def hop(self, dist):
        sub, last = self.sub, self.last
        pl.when(sub - dist >= 0)(lambda: self.from_line(sub - dist, self.right_s, sub < last, self.to_right))
        pl.when(sub + dist <= last)(lambda: self.from_line(sub + dist, self.left_s, sub > 0, self.to_left))
        if dist == 1:
            self.from_far(sub)
        else:
            pl.when(sub - dist + 1 >= 0)(lambda: self.from_far(sub - dist + 1))
            pl.when(sub + dist - 1 <= last)(lambda: self.from_far(sub + dist - 1))

    def end(self):
        sub, last, size = self.sub, self.last, self.sub_size
        pl.when(sub - last >= 0)(lambda: self.from_far(sub - last))
        pl.when(sub + last <= last)(lambda: self.from_far(sub + last))
        for src_sub in range(size):
            self.landed(self.ep_core * size + src_sub)
            self.landed(self.ep_diag * size + src_sub)
        for src_sub in range(size):
            self.sent(self.far_s, src_sub, self.to_far)
            self.sent(self.core_s, src_sub, self.to_core)
            self.sent(self.core_s, size + src_sub, self.to_core)
            pl.when((sub >= src_sub) & (sub < last))(lambda: self.sent(self.right_s, src_sub, self.to_right))
            pl.when((sub <= src_sub) & (sub > 0))(lambda: self.sent(self.left_s, src_sub, self.to_left))
        for a in range(self.count):
            pltpu.make_async_copy(self.stage[a], self.outs[a].at[self.me], self.loc.at[a]).wait()


def gather_scratch(arrays, num_dev, sub_size):
    sems = lambda n: pltpu.SemaphoreType.DMA((len(arrays), n))
    return [pltpu.VMEM(a.shape, a.dtype) for a in arrays] + [sems(num_dev), sems(sub_size), sems(sub_size), sems(sub_size), sems(2 * sub_size), pltpu.SemaphoreType.DMA((len(arrays),))]


def gather_body(count, sub_size, *refs):
    g = Gather(sub_size, refs[:count], refs[count:2 * count], refs[2 * count:3 * count], *refs[3 * count:])
    g.begin()
    for dist in range(1, sub_size):
        g.hop(dist)
    g.end()


def gather_tokens(arrays, num_dev, sub_size, collective_id):
    count = len(arrays)
    return pl.pallas_call(
        functools.partial(gather_body, count, sub_size),
        out_shape=[jax.ShapeDtypeStruct((num_dev,) + a.shape, a.dtype) for a in arrays],
        in_specs=[ANY] * count,
        out_specs=[ANY] * count,
        scratch_shapes=gather_scratch(arrays, num_dev, sub_size),
        compiler_params=pltpu.CompilerParams(collective_id=collective_id, has_side_effects=True, vmem_limit_bytes=VMEM_CAP),
        name='gather_tokens',
    )(*arrays)


FFN_STEPS = 4


def run_experts(mb, me, gath, metas, w1, w3, w2, rows, e_out, act_ref, after_pick, hook):
    num_dev, exp_local, cap_slots, dim = e_out.shape
    tok_count = gath.shape[1]
    top_k = metas.shape[2] // 2
    ff = w1.shape[2]
    room = exp_local * cap_slots
    steps = FFN_STEPS
    ft, nt = ff // steps, dim // steps
    base = (me * room).astype(jnp.float32)

    def pick(code_ref, tok_ref, out_ref):
        want = lax.broadcasted_iota(jnp.int32, (room, tok_count), 0).astype(jnp.float32) + base
        hit = code_ref[0, 0, 0:1, :] == want
        for j in range(1, top_k):
            hit = hit | (code_ref[0, 0, j:j + 1, :] == want)
        onehot = jnp.where(hit, 1.0, 0.0).astype(jnp.bfloat16)
        picked = jnp.dot(onehot, tok_ref[0], preferred_element_type=jnp.float32).astype(jnp.bfloat16)
        for e in range(exp_local):
            out_ref[e] = picked[e * cap_slots:(e + 1) * cap_slots]

    pltpu.emit_pipeline(
        pick,
        grid=(num_dev,),
        in_specs=[pl.BlockSpec((1, 1) + metas.shape[2:], lambda s: (s, mb, 0, 0)), pl.BlockSpec((1, tok_count, dim), lambda s: (s, 0, 0))],
        out_specs=[pl.BlockSpec((exp_local, cap_slots, dim), lambda s: (0, s, 0))],
    )(metas, gath, rows)
    after_pick()

    def ffn(indices, x_ref, w1_ref, w3_ref, w2_ref, out_ref):
        e, step = indices.index

        @pl.when(step < steps)
        def _():
            x = x_ref[0]
            gate_h = jnp.dot(x, w1_ref[0], preferred_element_type=jnp.float32)
            up_h = jnp.dot(x, w3_ref[0], preferred_element_type=jnp.float32)
            act_ref[step] = (jax.nn.silu(gate_h) * up_h).astype(jnp.bfloat16)

        @pl.when(step >= steps)
        def _():
            acc = jnp.dot(act_ref[0], w2_ref[0, 0:ft, :], preferred_element_type=jnp.float32)
            for k in range(1, steps):
                acc = acc + jnp.dot(act_ref[k], w2_ref[0, k * ft:(k + 1) * ft, :], preferred_element_type=jnp.float32)
            out_ref[...] = acc.astype(jnp.bfloat16).reshape(out_ref.shape)

        hook(e, step)

    pltpu.emit_pipeline(
        ffn,
        grid=(exp_local, 2 * steps),
        in_specs=[
            pl.BlockSpec((1, num_dev * cap_slots, dim), lambda e, s: (e, 0, 0)),
            pl.BlockSpec((1, dim, ft), lambda e, s: (e, 0, jnp.minimum(s, steps - 1))),
            pl.BlockSpec((1, dim, ft), lambda e, s: (e, 0, jnp.minimum(s, steps - 1))),
            pl.BlockSpec((1, ff, nt), lambda e, s: (e, 0, jnp.maximum(s - steps, 0))),
        ],
        out_specs=[pl.BlockSpec((num_dev, 1, cap_slots, nt), lambda e, s: (0, e, 0, jnp.maximum(s - steps, 0)))],
        _explicit_indices=True,
    )(rows, w1, w3, w2, e_out)


def expert_shapes(num_dev, exp_local, cap_slots, dim):
    return [jax.ShapeDtypeStruct((exp_local, num_dev * cap_slots, dim), jnp.bfloat16), jax.ShapeDtypeStruct((num_dev, exp_local, cap_slots, dim), jnp.bfloat16)]


def act_scratch(num_dev, cap_slots, ff):
    return pltpu.VMEM((FFN_STEPS, num_dev * cap_slots, ff // FFN_STEPS), jnp.bfloat16)


def first_body(sub_size, norm_b, gath_a, metas, w1, w3, w2, gath_b, rows, e_a, act_ref, stage, *sems):
    g = Gather(sub_size, [norm_b], [gath_b], [stage], *sems)
    g.begin()

    def hook(e, step):
        pl.when((e == 1) & (step == 4))(lambda: g.hop(2))
        pl.when((e == 3) & (step == 1))(lambda: g.hop(3))

    run_experts(0, g.me, gath_a, metas, w1, w3, w2, rows, e_a, act_ref, lambda: g.hop(1), hook)
    g.end()


def first_experts(norm_b, gath_a, metas, w1, w3, w2, cap_slots, sub_size, collective_id):
    num_dev, tok_count, dim = gath_a.shape
    exp_local, _, ff = w1.shape
    return pl.pallas_call(
        functools.partial(first_body, sub_size),
        out_shape=[jax.ShapeDtypeStruct(gath_a.shape, gath_a.dtype)] + expert_shapes(num_dev, exp_local, cap_slots, dim),
        in_specs=[ANY] * 6,
        out_specs=[ANY] * 3,
        scratch_shapes=[act_scratch(num_dev, cap_slots, ff)] + gather_scratch([norm_b], num_dev, sub_size),
        compiler_params=pltpu.CompilerParams(collective_id=collective_id, has_side_effects=True, vmem_limit_bytes=VMEM_CAP),
        name='first_experts',
    )(norm_b, gath_a, metas, w1, w3, w2)


PARTS = 2


class Combine:
    def __init__(self, mb, sub_size, e_ref, metas, hid, out, land, inbox, sums, mix, tile, a_recv, a_send, z_recv, z_send, loads):
        self.mb, self.sub_size, self.last = mb, sub_size, sub_size - 1
        self.e_ref, self.metas, self.hid, self.out, self.land = e_ref, metas, hid, out, land
        self.inbox, self.sums, self.mix, self.tile = inbox, sums, mix, tile
        self.a_recv, self.a_send, self.z_recv, self.z_send, self.loads = a_recv, a_send, z_recv, z_send, loads
        ep, sub = lax.axis_index('ep'), lax.axis_index('sub')
        self.ep, self.sub = ep, sub
        ep_far = lax.rem(ep + 2, 4)
        ep_core = ep + 1 - 2 * lax.rem(ep, 2)
        self.peers = [ep_far, lax.rem(ep_core + 2, 4), ep_core]
        self.to_right, self.to_left = {'ep': ep, 'sub': sub + 1}, {'ep': ep, 'sub': sub - 1}
        self.width = e_ref.shape[3] // PARTS

    def greet(self):
        greet(self.sub, self.sub_size, [{'ep': p, 'sub': self.sub} for p in self.peers], self.to_left, self.to_right)

    def order(self, i):
        side = self.sub // 2
        near = self.sub + side * (3 - 2 * self.sub)
        a = 3 - i + near * (3 * (i // 2) - 2 * ((i + 2) // 3))
        return a + side * (3 - 2 * a)

    def part(self, h):
        return pl.ds(pl.multiple_of(h * self.width, self.width), self.width)

    def slot_copy(self, dst, k, h, src_ep):
        return pltpu.make_async_remote_copy(
            src_ref=self.e_ref.at[self.peers[k] * self.sub_size + dst, :, :, self.part(h)], dst_ref=self.land.at[dst, src_ep, :, :, self.part(h)],
            send_sem=self.a_send.at[self.mb, dst, k, h], recv_sem=self.a_recv.at[self.mb, dst, src_ep, h], device_id={'ep': self.peers[k], 'sub': self.sub}, device_id_type=MESH)

    def line_copy(self, dst, h, box, dev):
        return pltpu.make_async_remote_copy(
            src_ref=self.sums.at[dst, :, self.part(h)], dst_ref=self.inbox.at[self.mb, box, :, self.part(h)],
            send_sem=self.z_send.at[self.mb, dst, h], recv_sem=self.z_recv.at[self.mb, box, h], device_id=dev, device_id_type=MESH)

    def begin(self):
        @pl.loop(0, self.sub_size * PARTS)
        def _(t):
            dst = self.order(t // PARTS)
            for k in range(3):
                self.slot_copy(dst, k, t % PARTS, self.ep).start()

    def build_mix(self, dst):
        tok_count, room = self.sums.shape[1], self.e_ref.shape[1] * self.e_ref.shape[2]
        cols = lax.broadcasted_iota(jnp.int32, (tok_count, 4 * room), 1)
        want = (cols + (cols // room) * ((self.sub_size - 1) * room) + self.sub * room).astype(jnp.float32)
        route = self.metas[self.ep * self.sub_size + dst, self.mb].T
        top_k = route.shape[1] // 2
        mat = jnp.zeros((tok_count, 4 * room), jnp.float32)
        for j in range(top_k):
            mat = jnp.where(route[:, j:j + 1] == want, route[:, top_k + j:top_k + j + 1], mat)
        for s in range(3):
            piece = mat.astype(jnp.bfloat16)
            self.mix[s * tok_count:(s + 1) * tok_count, :] = piece
            mat = mat - piece.astype(jnp.float32)

    def event(self, t):
        i, h = t // PARTS, t % PARTS
        dst, sub, last = self.order(i), self.sub, self.last
        tok_count = self.sums.shape[1]
        pl.when(h == 0)(lambda: self.build_mix(dst))
        for k in range(3):
            self.slot_copy(dst, k, h, self.peers[k]).wait_recv()
        pulls = [pltpu.make_async_copy(self.land.at[dst, p, :, :, self.part(h)], self.tile.at[p], self.loads.at[p]) for p in self.peers]
        pulls.append(pltpu.make_async_copy(self.e_ref.at[self.ep * self.sub_size + dst, :, :, self.part(h)], self.tile.at[self.ep], self.loads.at[self.ep]))
        for cp in pulls:
            cp.start()
        for cp in pulls:
            cp.wait()
        cut = 256

        @pl.loop(0, self.width // cut)
        def _(c):
            rows = self.tile[:, :, :, pl.ds(pl.multiple_of(c * cut, cut), cut)].reshape(self.mix.shape[1], cut)
            prod = jnp.dot(self.mix[...], rows, preferred_element_type=jnp.float32)
            self.sums[dst, :, pl.ds(pl.multiple_of(h * self.width + c * cut, cut), cut)] = prod[0:tok_count] + (prod[tok_count:2 * tok_count] + prod[2 * tok_count:])

        def add(box):
            self.line_copy(dst, h, box, self.to_left).wait_recv()
            self.sums[dst, :, self.part(h)] = self.sums[dst, :, self.part(h)] + self.inbox[self.mb, box, :, self.part(h)]

        size = self.sub_size
        pl.when((dst >= sub) & (sub > 0))(lambda: add(dst))
        pl.when((dst <= sub) & (sub < last))(lambda: add(dst + (1 - (sub - dst + last) // size) * (size - dst)))
        pl.when(dst > sub)(lambda: self.line_copy(dst, h, dst, self.to_right).start())
        pl.when(dst < sub)(lambda: self.line_copy(dst, h, dst + (1 - (sub - 1 - dst + last) // size) * (size - dst), self.to_left).start())

        @pl.when(dst == sub)
        def _():
            self.out[:, self.part(h)] = (self.hid[:, self.part(h)].astype(jnp.float32) + self.sums[dst, :, self.part(h)]).astype(jnp.bfloat16)

    def end(self):
        @pl.loop(0, self.sub_size * PARTS)
        def _(t):
            h = t % PARTS
            dst = self.order(t // PARTS)
            for k in range(3):
                self.slot_copy(dst, k, h, self.ep).wait_send()
            pl.when(dst != self.sub)(lambda: self.line_copy(dst, h, dst, self.to_right).wait_send())


def second_body(sub_size, e_a, gath_b, metas_any, w1, w3, w2, metas, hid_a, hid_b, out_a, out_b, land_a, land_b, rows, e_b, act_ref, inbox, sums, mix, tile, *sems):
    com_a = Combine(0, sub_size, e_a, metas, hid_a, out_a, land_a, inbox, sums, mix, tile, *sems)
    com_b = Combine(1, sub_size, e_b, metas, hid_b, out_b, land_b, inbox, sums, mix, tile, *sems)
    com_a.greet()
    com_a.begin()
    me = com_a.ep * sub_size + com_a.sub
    events = sub_size * PARTS

    def hook(e, step):
        pl.when(step == 2 * FFN_STEPS - 1)(lambda: com_a.event(e + 1))

    run_experts(1, me, gath_b, metas_any, w1, w3, w2, rows, e_b, act_ref, lambda: com_a.event(0), hook)
    com_b.begin()
    pl.loop(w1.shape[0] + 1, events)(com_a.event)
    com_a.end()
    pl.loop(0, events)(com_b.event)
    com_b.end()


def second_experts(e_a, gath_b, metas, w1, w3, w2, hid_a, hid_b, sub_size, collective_id):
    num_dev, exp_local, cap_slots, dim = e_a.shape
    tok_count = hid_a.shape[0]
    ff = w1.shape[2]
    room = exp_local * cap_slots
    dma = lambda *s: pltpu.SemaphoreType.DMA(s)
    land = jax.ShapeDtypeStruct((sub_size, 4, exp_local, cap_slots, dim), jnp.bfloat16)
    hid = jax.ShapeDtypeStruct((tok_count, dim), jnp.bfloat16)
    vmem = pl.BlockSpec(memory_space=pltpu.VMEM)
    return pl.pallas_call(
        functools.partial(second_body, sub_size),
        out_shape=[hid, hid, land, land] + expert_shapes(num_dev, exp_local, cap_slots, dim),
        in_specs=[ANY] * 6 + [vmem] * 3,
        out_specs=[vmem] * 2 + [ANY] * 4,
        scratch_shapes=[
            act_scratch(num_dev, cap_slots, ff),
            pltpu.VMEM((2, sub_size + 1, tok_count, dim), jnp.float32),
            pltpu.VMEM((sub_size, tok_count, dim), jnp.float32),
            pltpu.VMEM((3 * tok_count, 4 * room), jnp.bfloat16),
            pltpu.VMEM((4, exp_local, cap_slots, dim // PARTS), jnp.bfloat16),
            dma(2, sub_size, 4, PARTS), dma(2, sub_size, 3, PARTS), dma(2, sub_size + 1, PARTS), dma(2, sub_size, PARTS), dma(4),
        ],
        compiler_params=pltpu.CompilerParams(collective_id=collective_id, has_side_effects=True, vmem_limit_bytes=63 * 1024 * 1024),
        name='second_experts',
    )(e_a, gath_b, metas, w1, w3, w2, metas, hid_a, hid_b)


def solution(mesh):
    ep_size = mesh.shape['ep']
    sub_size = mesh.shape['sub']
    num_dev = ep_size * sub_size
    tok_spec = P(('dp', 'ep', 'sub'), None, None)
    route_spec = P(None, ('dp', 'ep', 'sub'), None)
    exp_spec = P(('ep', 'sub'), None, None)

    def device_body(input_a, input_b, route_idx, route_gate, attn_norm, w_query, w_key, w_value, w_out, moe_norm, w_gate, w_up, w_down):
        exp_local = w_gate.shape[0]
        num_exp = exp_local * num_dev
        tok_count, top_k = route_idx.shape[1:]
        dim = input_a.shape[2]
        cap_slots = 3 * top_k * tok_count // (2 * num_exp)

        meta = jnp.concatenate([jnp.stack([slot_codes(route_idx[m], num_exp, cap_slots) for m in range(2)]), route_gate], axis=2)
        meta = meta.transpose(0, 2, 1)
        hidden = [attention_block(x, attn_norm, w_query, w_key, w_value, w_out).reshape(tok_count, dim) for x in (input_a, input_b)]
        normed = [rms_norm(h, moe_norm) for h in hidden]
        gath_a, metas = gather_tokens([normed[0], meta], num_dev, sub_size, 1)
        gath_b, _, e_a = first_experts(normed[1], gath_a, metas, w_gate, w_up, w_down, cap_slots, sub_size, 2)
        outs = second_experts(e_a, gath_b, metas, w_gate, w_up, w_down, hidden[0], hidden[1], sub_size, 3)
        return outs[0].reshape(input_a.shape), outs[1].reshape(input_b.shape)

    return jax.shard_map(device_body, mesh=mesh, in_specs=(tok_spec, tok_spec, route_spec, route_spec, P(), P(), P(), P(), P(), P(), exp_spec, exp_spec, exp_spec), out_specs=(tok_spec, tok_spec), check_vma=False)
```

time: 1940 us -> 607 us (0.31)
  the two profiles are of different devices: /device:TPU:0 before, /device:TPU:16 now
where the time goes in v2:
time: 607 us; the launch traced here: 596 us
  Pallas kernels  514 us (85%)
  matrix products  53.5 us (9%)
  other arithmetic  21.9 us (4%)
    pallas_call x1, Pallas kernels, second_experts(): pl.pallas_call(functools.partial(second_body, sub_size), out_shape=[hid,...  306 us
    pallas_call x1, Pallas kernels, first_experts(): pl.pallas_call(functools.partial(first_body, sub_size), out_shape=[jax.Sh...  108 us
    pallas_call x1, Pallas kernels, gather_tokens(): pl.pallas_call(functools.partial(gather_body, count, sub_size), out_shape...  99.6 us
    dot_general x2, matrix products, attention_block(): jnp.einsum('bqhc,bkhc->bhqk', q_heads, k_heads, preferred_element_type=jn...  17.3 us
    dot_general x2, matrix products, attention_block(): jnp.einsum('crid,ide->cre', context, w_out, preferred_element_type=jnp.fl...  15.6 us
    sub x2, other arithmetic, attention_block(): prob_bf = jax.nn.softmax(scores, axis=-1).astype(jnp.bfloat16)  14.3 us

profile of v2, /device:TPU:16, one launch (start us, length us, event | category | flops | bytes accessed | tf_op | source)
XLA Modules:
  0.0 596.2 jit_solution(8331700587132921297)
XLA Ops:
  0.6 1.5 fusion.29
  2.1 1.5 fusion.26
  3.7 0.7 slice_bitcast_fusion.1
  4.5 0.2 fusion.72
  4.7 0.2 fusion.73
  4.9 0.2 select_reduce_fusion
  5.1 0.9 bitcast_add_fusion.1
  6.0 1.4 maximum_bitcast_fusion.refs_1_
  7.4 7.3 %fusion.60 = bf16[256,16,128]{2,0,1:T(8,128)(2,1)} fusion(bf16[2048,16,128]{2,1,0:T(8,128)(2,1)} %param.19, bf16[1,256,2048]{2,1,0:T(8,128)(2,1)} %param.14, f32[2048]{0:T(1024)} %param.17, f32[256]{0:T(256)S(1)} %add_rsqrt_fusion.3), kind=kOutput, calls=%fused_computation.66 | convolution fusion | flops 2150105088 | bytes 10494976 | tf_op jit(solution)/shard_map/bsd,dhc->bshc/dot_general | solution.py:25
  14.7 5.2 fusion.42
  19.9 2.4 fusion.63
  22.4 5.4 fusion.45
  27.7 8.3 %fusion.58 = f32[16,256,256]{1,2,0:T(8,128)} fusion(bf16[256,16,128]{2,0,1:T(8,128)(2,1)S(1)} %fusion.63, bf16[2048,16,128]{2,1,0:T(8,128)(2,1)} %param.18, bf16[1,256,2048]{2,1,0:T(8,128)(2,1)S(1)} %copy-done.2, f32[256]{0:T(256)S(1)} %add_rsqrt_fusion.1, f32[2048]{0:T(1024)S(1)} %copy-done.6), kind=kOutput, calls=%fused_computation.65 | convolution fusion | flops 2418540544 | bytes 14689280 | tf_op jit(solution)/shard_map/bqhc,bkhc->bhqk/dot_general | solution.py:28
  36.1 7.1 %fusion.86 = (f32[16,256]{1,0:T(8,128)S(1)}, f32[16,256,256]{1,2,0:T(8,128)}) fusion(f32[16,256,256]{1,2,0:T(8,128)} %fusion.58, pred[256,256]{0,1:T(8,128)(4,1)S(1)} %iota_compare_fusion.5), kind=kOutput, calls=%fused_computation.95 | output fusion | flops 6291711 | bytes 8470528 | tf_op jit(solution)/shard_map/sub | solution.py:32
  43.1 7.8 %fusion.23 = (f32[256]{0:T(256)S(1)}, bf16[256,2048]{1,0:T(8,128)(2,1)S(1)}) fusion(bf16[16,128,2048]{2,1,0:T(8,128)(2,1)} %param.21, bf16[256,16,128]{0,2,1:T(8,128)(2,1)} %fusion.45, f32[16,256,256]{1,2,0:T(8,128)} %get-tuple-element.21, f32[16,256]{1,0:T(8,128)S(1)} %get-tuple-element.20, bf16[1,256,2048]{2,1,0:T(8,128)(2,1)S(1)} %copy-done.2), kind=kOutput, calls=%fused_computation.41 | convolution fusion | flops 2421686016 | bytes 15746048 | tf_op jit(solution)/shard_map/crid,ide->cre/dot_general | solution.py:34
  50.9 9.0 %fusion.52 = f32[16,256,256]{1,2,0:T(8,128)} fusion(bf16[256,16,128]{2,0,1:T(8,128)(2,1)} %fusion.60, bf16[2048,16,128]{2,1,0:T(8,128)(2,1)} %param.18, bf16[1,256,2048]{2,1,0:T(8,128)(2,1)S(1)} %copy-done.3, f32[2048]{0:T(1024)S(1)} %copy-done.6, f32[256]{0:T(256)S(1)} %add_rsqrt_fusion.3), kind=kOutput, calls=%fused_computation.63 | convolution fusion | flops 2418540544 | bytes 14689280 | tf_op jit(solution)/shard_map/bqhc,bkhc->bhqk/dot_general | solution.py:28
  59.9 7.3 %fusion.87 = (f32[16,256]{1,0:T(8,128)S(1)}, f32[16,256,256]{1,2,0:T(8,128)}) fusion(f32[16,256,256]{1,2,0:T(8,128)} %fusion.52, pred[256,256]{0,1:T(8,128)(4,1)S(1)} %iota_compare_fusion.5), kind=kOutput, calls=%fused_computation.96 | output fusion | flops 6291711 | bytes 8470528 | tf_op jit(solution)/shard_map/sub | solution.py:32
  67.2 7.8 %fusion.20 = (f32[256]{0:T(256)S(1)}, bf16[256,2048]{1,0:T(8,128)(2,1)S(1)}) fusion(bf16[16,128,2048]{2,1,0:T(8,128)(2,1)} %param.21, bf16[256,16,128]{0,2,1:T(8,128)(2,1)} %fusion.42, f32[16,256,256]{1,2,0:T(8,128)} %get-tuple-element.25, f32[16,256]{1,0:T(8,128)S(1)} %get-tuple-element.24, bf16[1,256,2048]{2,1,0:T(8,128)(2,1)S(1)} %copy-done.3), kind=kOutput, calls=%fused_computation.38 | convolution fusion | flops 2421686016 | bytes 15746048 | tf_op jit(solution)/shard_map/crid,ide->cre/dot_general | solution.py:34
  75.0 1.9 fusion.25
  76.9 99.6 %gather_tokens.1 = (bf16[16,256,2048]{2,1,0:T(8,128)(2,1)}, f32[16,2,16,256]{3,2,1,0:T(8,128)}) custom-call(bf16[256,2048]{1,0:T(8,128)(2,1)} %get-tuple-element.18.refs_0_, f32[2,16,256]{2,1,0:T(8,128)} %maximum_bitcast_fusion.refs_1_), custom_call_target="tpu_custom_call" | custom-call | tf_op jit(solution)/shard_map/gather_tokens/pallas_call | solution.py:161
  176.5 108.5 %first_experts.1 = (bf16[16,256,2048]{2,1,0:T(8,128)(2,1)}, bf16[4,768,2048]{2,1,0:T(8,128)(2,1)}, bf16[16,4,48,2048]{3,2,1,0:T(8,128)(2,1)}) custom-call(bf16[256,2048]{1,0:T(8,128)(2,1)} %get-tuple-element.19.norm_b, bf16[16,256,2048]{2,1,0:T(8,128)(2,1)} %get-tuple-element.8.gath_a, f32[16,2,16,256]{3,2,1,0:T(8,128)} %get-tuple-element.9.metas.metas_any, ...), custom_call_target="tpu_custom_call" | custom-call | tf_op jit(solution)/shard_map/first_experts/pallas_call | solution.py:259
  285.0 306.1 %second_experts.1 = (bf16[256,2048]{1,0:T(8,128)(2,1)}, bf16[256,2048]{1,0:T(8,128)(2,1)}, bf16[4,4,4,48,2048]{4,3,2,1,0:T(8,128)(2,1)}, bf16[4,4,4,48,2048]{4,3...) custom-call(bf16[16,4,48,2048]{3,2,1,0:T(8,128)(2,1)} %get-tuple-element.10.e_a, ...), custom_call_target="tpu_custom_call" | custom-call | tf_op jit(solution)/shard_map/second_experts/pallas_call | solution.py:403
  591.1 2.3 copy.64
  593.4 2.3 copy.65
  (25 shorter events, 0.2 us)
Async XLA Ops:
  4.7 15.2 %slice-start = ((s8[8388608]{0:T(1024)(128)(4,1)}), s8[4194304]{0:T(1024)(128)(4,1)S(1)}, s32[]{:S(2)}) async-start(s8[8388608]{0:T(1024)(128)(4,1)} %bitcast.78), calls=%async_computation | async-start | bytes 8388608
  7.4 7.3 %copy-start.3 = (bf16[1,256,2048]{2,1,0:T(8,128)(2,1)S(1)}, bf16[1,256,2048]{2,1,0:T(8,128)(2,1)}, u32[]{:S(2)}) copy-start(bf16[1,256,2048]{2,1,0:T(8,128)(2,1)} %param.14) | copy-start | bytes 3145732
  7.4 7.3 %copy-start.5 = (bf16[2048,16,128]{2,1,0:T(8,128)(2,1)S(1)}, bf16[2048,16,128]{2,1,0:T(8,128)(2,1)}, u32[]{:S(2)}) copy-start(bf16[2048,16,128]{2,1,0:T(8,128)(2,1)} %param.20) | copy-start | bytes 25165828
  7.4 7.3 %copy-start.6 = (f32[2048]{0:T(1024)S(1)}, f32[2048]{0:T(1024)}, u32[]{:S(2)}) copy-start(f32[2048]{0:T(1024)} %param.17) | copy-start | bytes 24580
  7.4 12.5 %slice-start.1 = ((s8[8388608]{0:T(1024)(128)(4,1)}), s8[4194304]{0:T(1024)(128)(4,1)S(1)}, s32[]{:S(2)}) async-start(s8[8388608]{0:T(1024)(128)(4,1)} %bitcast.78), calls=%async_computation.1 | async-start | bytes 8388608
  14.7 5.2 copy-start.2
  50.9 24.1 %copy-start = (bf16[256,2048]{1,0:T(8,128)(2,1)}, bf16[256,2048]{1,0:T(8,128)(2,1)S(1)}, u32[]{:S(2)}) copy-start(bf16[256,2048]{1,0:T(8,128)(2,1)S(1)} %get-tuple-element.23.hid_a) | copy-start | bytes 3145732
  67.2 7.8 %copy-start.4 = (f32[2048]{0:T(1024)S(1)}, f32[2048]{0:T(1024)}, u32[]{:S(2)}) copy-start(f32[2048]{0:T(1024)} %param.22) | copy-start | bytes 24580
  75.0 210.0 %copy-start.1 = (bf16[256,2048]{1,0:T(8,128)(2,1)}, bf16[256,2048]{1,0:T(8,128)(2,1)S(1)}, u32[]{:S(2)}) copy-start(bf16[256,2048]{1,0:T(8,128)(2,1)S(1)} %get-tuple-element.27.hid_b) | copy-start | bytes 3145732

commit v3 on v2

--- a/solution.py
+++ b/solution.py
@@ -9,7 +9,7 @@
 
 NORM_EPS = 1e-6
 MESH = pl.DeviceIdType.MESH
-VMEM_CAP = 60 * 1024 * 1024
+VMEM_CAP = 63 * 1024 * 1024
 ANY = pl.BlockSpec(memory_space=pl.ANY)
 
 
@@ -19,20 +19,42 @@
     return (acc_f32 * inv_rms * norm_gain).astype(jnp.bfloat16)
 
 
-def attention_block(tokens, attn_norm, w_query, w_key, w_value, w_out):
-    normed = rms_norm(tokens, attn_norm)
-    q_heads = jnp.einsum('bsd,dhc->bshc', normed, w_query, preferred_element_type=jnp.float32).astype(jnp.bfloat16)
-    k_heads = jnp.einsum('bsd,dhc->bshc', normed, w_key, preferred_element_type=jnp.float32).astype(jnp.bfloat16)
-    v_heads = jnp.einsum('bsd,dhc->bshc', normed, w_value, preferred_element_type=jnp.float32).astype(jnp.bfloat16)
-    score_scale = w_query.shape[2] ** -0.5
-    scores = jnp.einsum('bqhc,bkhc->bhqk', q_heads, k_heads, preferred_element_type=jnp.float32) * score_scale
-    seq_len = tokens.shape[1]
-    causal = lax.broadcasted_iota(jnp.int32, (seq_len, seq_len), 0) >= lax.broadcasted_iota(jnp.int32, (seq_len, seq_len), 1)
-    scores = jnp.where(causal, scores, -jnp.inf)
-    prob_bf = jax.nn.softmax(scores, axis=-1).astype(jnp.bfloat16)
-    context = jnp.einsum('bhqk,bkhc->bqhc', prob_bf, v_heads, preferred_element_type=jnp.float32).astype(jnp.bfloat16)
-    proj_out = jnp.einsum('crid,ide->cre', context, w_out, preferred_element_type=jnp.float32)
-    return (tokens.astype(jnp.float32) + proj_out).astype(jnp.bfloat16)
+HEADS_STEP = 2
+
+
+def attend(mb, q, k, v, x, w_out, gain, hid, normed, sem):
+    num_heads, seq_len, head_dim = q.shape[1:]
+    dim = hid.shape[1]
+    load = pltpu.make_async_copy(x.at[0], hid, sem)
+    load.start()
+
+    def body(ctx):
+        causal = lax.broadcasted_iota(jnp.int32, (seq_len, seq_len), 0) >= lax.broadcasted_iota(jnp.int32, (seq_len, seq_len), 1)
+
+        def heads(indices, q_ref, k_ref, v_ref):
+            n, = indices.index
+            for h in range(HEADS_STEP):
+                scores = lax.dot_general(q_ref[0, h], k_ref[0, h], (((1,), (1,)), ((), ())), preferred_element_type=jnp.float32) * head_dim ** -0.5
+                scores = jnp.where(causal, scores, -jnp.inf)
+                weights = jnp.exp(scores - jnp.max(scores, axis=-1, keepdims=True))
+                prob = (weights / jnp.sum(weights, axis=-1, keepdims=True)).astype(jnp.bfloat16)
+                out = jnp.dot(prob, v_ref[0, h], preferred_element_type=jnp.float32).astype(jnp.bfloat16)
+                ctx[:, pl.ds(pl.multiple_of((n * HEADS_STEP + h) * head_dim, head_dim), head_dim)] = out
+
+        spec = pl.BlockSpec((1, HEADS_STEP, seq_len, head_dim), lambda n: (mb, n, 0, 0))
+        pltpu.emit_pipeline(heads, grid=(num_heads // HEADS_STEP,), in_specs=[spec] * 3, _explicit_indices=True)(q, k, v)
+        load.wait()
+        cut = 512
+
+        def project(indices, w_ref):
+            n, = indices.index
+            cols = pl.ds(pl.multiple_of(n * cut, cut), cut)
+            hid[:, cols] = (hid[:, cols].astype(jnp.float32) + jnp.dot(ctx[...], w_ref[...], preferred_element_type=jnp.float32)).astype(jnp.bfloat16)
+
+        pltpu.emit_pipeline(project, grid=(dim // cut,), in_specs=[pl.BlockSpec((w_out.shape[0], cut), lambda n: (0, n))], _explicit_indices=True)(w_out)
+        normed[...] = rms_norm(hid[...], gain[...])
+
+    pl.run_scoped(body, pltpu.VMEM((seq_len, num_heads * head_dim), jnp.bfloat16))
 
 
 def slot_codes(exp_ids, num_exp, cap_slots):
@@ -57,6 +79,20 @@
     pl.when(sub > 0)(lambda: hello(to_left))
     pl.when(sub < last)(lambda: hello(to_right))
     pl.semaphore_wait(barrier, len(peers) + (sub + last) // sub_size + (2 * last - sub) // sub_size)
+
+
+def at_rank(sub, k):
+    side = sub // 2
+    near = sub + side * (3 - 2 * sub)
+    a = k + near * (1 - k // 2) * (1 - 2 * k)
+    return a + side * (3 - 2 * a)
+
+
+def rank_of(sub, place):
+    side = sub // 2
+    near = sub + side * (3 - 2 * sub)
+    a = place + side * (3 - 2 * place)
+    return a + near * (1 - a // 2) * (1 - 2 * a)
 
 
 class Gather:
@@ -85,23 +121,26 @@
             cp.wait_recv()
 
     def sent(self, sem, slot, dev):
-        for cp in self.copies(lambda a: self.ins[a], 0, sem, slot, dev):
+        for cp in self.copies(lambda a: self.outs[a].at[self.me], 0, sem, slot, dev):
             cp.wait_send()
 
     def begin(self):
-        own = lambda a: self.ins[a]
         sub, me = self.sub, self.me
-        greet(sub, self.sub_size, [self.to_far, self.to_core], self.to_left, self.to_right)
+        own = lambda a: self.outs[a].at[me]
+        for a in range(self.count):
+            if self.ins[a] is not None:
+                cp = pltpu.make_async_copy(self.ins[a], self.stage[a], self.loc.at[a])
+                cp.start()
+                cp.wait()
+        keep = [pltpu.make_async_copy(self.stage[a], own(a), self.loc.at[a]) for a in range(self.count)]
+        for cp in keep:
+            cp.start()
+        for cp in keep:
+            cp.wait()
         pl.when(sub < self.last)(lambda: self.start(own, me, self.right_s, sub, self.to_right))
         pl.when(sub > 0)(lambda: self.start(own, me, self.left_s, sub, self.to_left))
         self.start(own, me, self.far_s, sub, self.to_far)
         self.start(own, me, self.core_s, sub, self.to_core)
-        for a in range(self.count):
-            cp = pltpu.make_async_copy(self.ins[a], self.stage[a], self.loc.at[a])
-            cp.start()
-            cp.wait()
-        for a in range(self.count):
-            pltpu.make_async_copy(self.stage[a], self.outs[a].at[me], self.loc.at[a]).start()
 
     def from_far(self, src_sub):
         blk = self.ep_far * self.sub_size + src_sub
@@ -126,21 +165,25 @@
             pl.when(sub - dist + 1 >= 0)(lambda: self.from_far(sub - dist + 1))
             pl.when(sub + dist - 1 <= last)(lambda: self.from_far(sub + dist - 1))
 
-    def end(self):
-        sub, last, size = self.sub, self.last, self.sub_size
+    def core_ready(self, first, stop):
+        for k in range(first, stop):
+            src_sub = at_rank(self.sub, k)
+            self.landed(self.ep_core * self.sub_size + src_sub)
+            self.landed(self.ep_diag * self.sub_size + src_sub)
+
+    def last_far(self):
+        sub, last = self.sub, self.last
         pl.when(sub - last >= 0)(lambda: self.from_far(sub - last))
         pl.when(sub + last <= last)(lambda: self.from_far(sub + last))
-        for src_sub in range(size):
-            self.landed(self.ep_core * size + src_sub)
-            self.landed(self.ep_diag * size + src_sub)
+
+    def drain(self):
+        sub, last, size = self.sub, self.last, self.sub_size
         for src_sub in range(size):
             self.sent(self.far_s, src_sub, self.to_far)
             self.sent(self.core_s, src_sub, self.to_core)
             self.sent(self.core_s, size + src_sub, self.to_core)
             pl.when((sub >= src_sub) & (sub < last))(lambda: self.sent(self.right_s, src_sub, self.to_right))
             pl.when((sub <= src_sub) & (sub > 0))(lambda: self.sent(self.left_s, src_sub, self.to_left))
-        for a in range(self.count):
-            pltpu.make_async_copy(self.stage[a], self.outs[a].at[self.me], self.loc.at[a]).wait()
 
 
 def gather_scratch(arrays, num_dev, sub_size):
@@ -148,39 +191,23 @@
     return [pltpu.VMEM(a.shape, a.dtype) for a in arrays] + [sems(num_dev), sems(sub_size), sems(sub_size), sems(sub_size), sems(2 * sub_size), pltpu.SemaphoreType.DMA((len(arrays),))]
 
 
-def gather_body(count, sub_size, *refs):
-    g = Gather(sub_size, refs[:count], refs[count:2 * count], refs[2 * count:3 * count], *refs[3 * count:])
-    g.begin()
-    for dist in range(1, sub_size):
-        g.hop(dist)
-    g.end()
-
-
-def gather_tokens(arrays, num_dev, sub_size, collective_id):
-    count = len(arrays)
-    return pl.pallas_call(
-        functools.partial(gather_body, count, sub_size),
-        out_shape=[jax.ShapeDtypeStruct((num_dev,) + a.shape, a.dtype) for a in arrays],
-        in_specs=[ANY] * count,
-        out_specs=[ANY] * count,
-        scratch_shapes=gather_scratch(arrays, num_dev, sub_size),
-        compiler_params=pltpu.CompilerParams(collective_id=collective_id, has_side_effects=True, vmem_limit_bytes=VMEM_CAP),
-        name='gather_tokens',
-    )(*arrays)
-
-
 FFN_STEPS = 4
 
 
-def run_experts(mb, me, gath, metas, w1, w3, w2, rows, e_out, act_ref, after_pick, hook):
-    num_dev, exp_local, cap_slots, dim = e_out.shape
-    tok_count = gath.shape[1]
+HALVES = 2
+
+
+def pick_rows(mb, half, ep, sub, sub_size, gath, metas, rows, exp_local, cap_slots):
+    num_dev, tok_count, dim = gath.shape
     top_k = metas.shape[2] // 2
-    ff = w1.shape[2]
     room = exp_local * cap_slots
-    steps = FFN_STEPS
-    ft, nt = ff // steps, dim // steps
-    base = (me * room).astype(jnp.float32)
+    blocks = num_dev // HALVES
+    ep_size = num_dev // sub_size
+    base = ((ep * sub_size + sub) * room).astype(jnp.float32)
+
+    def block(p):
+        q = half * blocks + p
+        return (q % ep_size) * sub_size + at_rank(sub, q // ep_size)
 
     def pick(code_ref, tok_ref, out_ref):
         want = lax.broadcasted_iota(jnp.int32, (room, tok_count), 0).astype(jnp.float32) + base
@@ -194,11 +221,17 @@
 
     pltpu.emit_pipeline(
         pick,
-        grid=(num_dev,),
-        in_specs=[pl.BlockSpec((1, 1) + metas.shape[2:], lambda s: (s, mb, 0, 0)), pl.BlockSpec((1, tok_count, dim), lambda s: (s, 0, 0))],
-        out_specs=[pl.BlockSpec((exp_local, cap_slots, dim), lambda s: (0, s, 0))],
+        grid=(blocks,),
+        in_specs=[pl.BlockSpec((1, 1) + metas.shape[2:], lambda p: (block(p), mb, 0, 0)), pl.BlockSpec((1, tok_count, dim), lambda p: (block(p), 0, 0))],
+        out_specs=[pl.BlockSpec((exp_local, cap_slots, dim), lambda p: (0, half * blocks + p, 0))],
     )(metas, gath, rows)
-    after_pick()
+
+
+def run_experts(w1, w3, w2, rows, e_out, act_ref, hook):
+    num_dev, exp_local, cap_slots, dim = e_out.shape
+    ff = w1.shape[2]
+    steps = FFN_STEPS
+    ft, nt = ff // steps, dim // steps
 
     def ffn(indices, x_ref, w1_ref, w3_ref, w2_ref, out_ref):
         e, step = indices.index
@@ -231,40 +264,6 @@
         out_specs=[pl.BlockSpec((num_dev, 1, cap_slots, nt), lambda e, s: (0, e, 0, jnp.maximum(s - steps, 0)))],
         _explicit_indices=True,
     )(rows, w1, w3, w2, e_out)
-
-
-def expert_shapes(num_dev, exp_local, cap_slots, dim):
-    return [jax.ShapeDtypeStruct((exp_local, num_dev * cap_slots, dim), jnp.bfloat16), jax.ShapeDtypeStruct((num_dev, exp_local, cap_slots, dim), jnp.bfloat16)]
-
-
-def act_scratch(num_dev, cap_slots, ff):
-    return pltpu.VMEM((FFN_STEPS, num_dev * cap_slots, ff // FFN_STEPS), jnp.bfloat16)
-
-
-def first_body(sub_size, norm_b, gath_a, metas, w1, w3, w2, gath_b, rows, e_a, act_ref, stage, *sems):
-    g = Gather(sub_size, [norm_b], [gath_b], [stage], *sems)
-    g.begin()
-
-    def hook(e, step):
-        pl.when((e == 1) & (step == 4))(lambda: g.hop(2))
-        pl.when((e == 3) & (step == 1))(lambda: g.hop(3))
-
-    run_experts(0, g.me, gath_a, metas, w1, w3, w2, rows, e_a, act_ref, lambda: g.hop(1), hook)
-    g.end()
-
-
-def first_experts(norm_b, gath_a, metas, w1, w3, w2, cap_slots, sub_size, collective_id):
-    num_dev, tok_count, dim = gath_a.shape
-    exp_local, _, ff = w1.shape
-    return pl.pallas_call(
-        functools.partial(first_body, sub_size),
-        out_shape=[jax.ShapeDtypeStruct(gath_a.shape, gath_a.dtype)] + expert_shapes(num_dev, exp_local, cap_slots, dim),
-        in_specs=[ANY] * 6,
-        out_specs=[ANY] * 3,
-        scratch_shapes=[act_scratch(num_dev, cap_slots, ff)] + gather_scratch([norm_b], num_dev, sub_size),
-        compiler_params=pltpu.CompilerParams(collective_id=collective_id, has_side_effects=True, vmem_limit_bytes=VMEM_CAP),
-        name='first_experts',
-    )(norm_b, gath_a, metas, w1, w3, w2)
 
 
 PARTS = 2
@@ -298,7 +297,7 @@
 
     def slot_copy(self, dst, k, h, src_ep):
         return pltpu.make_async_remote_copy(
-            src_ref=self.e_ref.at[self.peers[k] * self.sub_size + dst, :, :, self.part(h)], dst_ref=self.land.at[dst, src_ep, :, :, self.part(h)],
+            src_ref=self.e_ref.at[rank_of(self.sub, dst) * 4 + self.peers[k], :, :, self.part(h)], dst_ref=self.land.at[dst, src_ep, :, :, self.part(h)],
             send_sem=self.a_send.at[self.mb, dst, k, h], recv_sem=self.a_recv.at[self.mb, dst, src_ep, h], device_id={'ep': self.peers[k], 'sub': self.sub}, device_id_type=MESH)
 
     def line_copy(self, dst, h, box, dev):
@@ -317,7 +316,7 @@
         tok_count, room = self.sums.shape[1], self.e_ref.shape[1] * self.e_ref.shape[2]
         cols = lax.broadcasted_iota(jnp.int32, (tok_count, 4 * room), 1)
         want = (cols + (cols // room) * ((self.sub_size - 1) * room) + self.sub * room).astype(jnp.float32)
-        route = self.metas[self.ep * self.sub_size + dst, self.mb].T
+        route = self.metas[dst, self.mb].T
         top_k = route.shape[1] // 2
         mat = jnp.zeros((tok_count, 4 * room), jnp.float32)
         for j in range(top_k):
@@ -335,7 +334,7 @@
         for k in range(3):
             self.slot_copy(dst, k, h, self.peers[k]).wait_recv()
         pulls = [pltpu.make_async_copy(self.land.at[dst, p, :, :, self.part(h)], self.tile.at[p], self.loads.at[p]) for p in self.peers]
-        pulls.append(pltpu.make_async_copy(self.e_ref.at[self.ep * self.sub_size + dst, :, :, self.part(h)], self.tile.at[self.ep], self.loads.at[self.ep]))
+        pulls.append(pltpu.make_async_copy(self.e_ref.at[rank_of(self.sub, dst) * 4 + self.ep, :, :, self.part(h)], self.tile.at[self.ep], self.loads.at[self.ep]))
         for cp in pulls:
             cp.start()
         for cp in pulls:
@@ -372,50 +371,97 @@
             pl.when(dst != self.sub)(lambda: self.line_copy(dst, h, dst, self.to_right).wait_send())
 
 
-def second_body(sub_size, e_a, gath_b, metas_any, w1, w3, w2, metas, hid_a, hid_b, out_a, out_b, land_a, land_b, rows, e_b, act_ref, inbox, sums, mix, tile, *sems):
-    com_a = Combine(0, sub_size, e_a, metas, hid_a, out_a, land_a, inbox, sums, mix, tile, *sems)
-    com_b = Combine(1, sub_size, e_b, metas, hid_b, out_b, land_b, inbox, sums, mix, tile, *sems)
-    com_a.greet()
-    com_a.begin()
-    me = com_a.ep * sub_size + com_a.sub
+def layer_body(sub_size, q, k, v, x_a, x_b, w_out, meta, w1, w3, w2, gain, out_a, out_b, gath_a, gath_b, metas, rows_a, rows_b, e_a, e_b, land_a, land_b,
+               act_ref, near_meta, hid_a, hid_b, x_sem, inbox, sums, mix, tile, meta_sem, a_recv, a_send, z_recv, z_send, loads, stage_a, stage_m, *rest):
+    sems_a, stage_b, sems_b = rest[:6], rest[6], rest[7:]
+    ga = Gather(sub_size, [None, meta], [gath_a, metas], [stage_a, stage_m], *sems_a)
+    gb = Gather(sub_size, [None], [gath_b], [stage_b], *sems_b)
+    sems = (a_recv, a_send, z_recv, z_send, loads)
+    ca = Combine(0, sub_size, e_a, near_meta, hid_a, out_a, land_a, inbox, sums, mix, tile, *sems)
+    cb = Combine(1, sub_size, e_b, near_meta, hid_b, out_b, land_b, inbox, sums, mix, tile, *sems)
+    ep, sub = ca.ep, ca.sub
+    weights = (w1, w3, w2)
     events = sub_size * PARTS
 
-    def hook(e, step):
-        pl.when(step == 2 * FFN_STEPS - 1)(lambda: com_a.event(e + 1))
-
-    run_experts(1, me, gath_b, metas_any, w1, w3, w2, rows, e_b, act_ref, lambda: com_a.event(0), hook)
-    com_b.begin()
-    pl.loop(w1.shape[0] + 1, events)(com_a.event)
-    com_a.end()
-    pl.loop(0, events)(com_b.event)
-    com_b.end()
-
-
-def second_experts(e_a, gath_b, metas, w1, w3, w2, hid_a, hid_b, sub_size, collective_id):
-    num_dev, exp_local, cap_slots, dim = e_a.shape
-    tok_count = hid_a.shape[0]
-    ff = w1.shape[2]
+    def at(e, step, when_e, when_step, fn):
+        pl.when((e == when_e) & (step == when_step))(fn)
+
+    def pick(mb, half):
+        pick_rows(mb, half, ep, sub, sub_size, (gath_a, gath_b)[mb], metas, (rows_a, rows_b)[mb], w1.shape[0], e_a.shape[2])
+
+    def hook_a(e, step):
+        at(e, step, 0, 0, lambda: gb.hop(2))
+        at(e, step, 1, 4, lambda: gb.hop(3))
+
+    def hook_b(e, step):
+        pl.when(step == 2 * FFN_STEPS - 1)(lambda: ca.event(e + 1))
+
+    ca.greet()
+    attend(0, q, k, v, x_a, w_out, gain, hid_a, stage_a, x_sem)
+    ga.begin()
+    attend(1, q, k, v, x_b, w_out, gain, hid_b, stage_b, x_sem)
+    ga.hop(1)
+    ga.hop(2)
+    ga.core_ready(0, 2)
+    pick(0, 0)
+    ga.hop(3)
+    gb.begin()
+    ga.last_far()
+    ga.core_ready(2, 4)
+    gb.hop(1)
+    pick(0, 1)
+    run_experts(*weights, rows_a, e_a, act_ref, hook_a)
+    ca.begin()
+    pull = pltpu.make_async_copy(metas.at[pl.ds(ep * sub_size, sub_size)], near_meta, meta_sem)
+    pull.start()
+    pull.wait()
+    gb.core_ready(0, 2)
+    pick(1, 0)
+    gb.last_far()
+    gb.core_ready(2, 4)
+    pick(1, 1)
+    ca.event(0)
+    run_experts(*weights, rows_b, e_b, act_ref, hook_b)
+    cb.begin()
+    pl.loop(w1.shape[0] + 1, events)(ca.event)
+    ca.end()
+    pl.loop(0, events)(cb.event)
+    cb.end()
+    ga.drain()
+    gb.drain()
+
+
+def run_layer(q, k, v, x_a, x_b, w_out, meta, w1, w3, w2, gain, num_dev, cap_slots, sub_size):
+    _, tok_count, dim = x_a.shape
+    exp_local, _, ff = w1.shape
     room = exp_local * cap_slots
     dma = lambda *s: pltpu.SemaphoreType.DMA(s)
-    land = jax.ShapeDtypeStruct((sub_size, 4, exp_local, cap_slots, dim), jnp.bfloat16)
-    hid = jax.ShapeDtypeStruct((tok_count, dim), jnp.bfloat16)
+    bf = lambda *s: jax.ShapeDtypeStruct(s, jnp.bfloat16)
+    hid, gath = bf(tok_count, dim), bf(num_dev, tok_count, dim)
+    land = bf(sub_size, 4, exp_local, cap_slots, dim)
+    rows, e_out = bf(exp_local, num_dev * cap_slots, dim), bf(num_dev, exp_local, cap_slots, dim)
     vmem = pl.BlockSpec(memory_space=pltpu.VMEM)
     return pl.pallas_call(
-        functools.partial(second_body, sub_size),
-        out_shape=[hid, hid, land, land] + expert_shapes(num_dev, exp_local, cap_slots, dim),
-        in_specs=[ANY] * 6 + [vmem] * 3,
-        out_specs=[vmem] * 2 + [ANY] * 4,
+        functools.partial(layer_body, sub_size),
+        out_shape=[hid, hid, gath, gath, jax.ShapeDtypeStruct((num_dev,) + meta.shape, meta.dtype), rows, rows, e_out, e_out, land, land],
+        in_specs=[ANY] * 10 + [vmem],
+        out_specs=[vmem] * 2 + [ANY] * 9,
         scratch_shapes=[
-            act_scratch(num_dev, cap_slots, ff),
+            pltpu.VMEM((FFN_STEPS, num_dev * cap_slots, ff // FFN_STEPS), jnp.bfloat16),
+            pltpu.VMEM((sub_size,) + meta.shape, meta.dtype),
+            pltpu.VMEM((tok_count, dim), jnp.bfloat16),
+            pltpu.VMEM((tok_count, dim), jnp.bfloat16),
+            pltpu.SemaphoreType.DMA,
             pltpu.VMEM((2, sub_size + 1, tok_count, dim), jnp.float32),
             pltpu.VMEM((sub_size, tok_count, dim), jnp.float32),
             pltpu.VMEM((3 * tok_count, 4 * room), jnp.bfloat16),
             pltpu.VMEM((4, exp_local, cap_slots, dim // PARTS), jnp.bfloat16),
+            pltpu.SemaphoreType.DMA,
             dma(2, sub_size, 4, PARTS), dma(2, sub_size, 3, PARTS), dma(2, sub_size + 1, PARTS), dma(2, sub_size, PARTS), dma(4),
-        ],
-        compiler_params=pltpu.CompilerParams(collective_id=collective_id, has_side_effects=True, vmem_limit_bytes=63 * 1024 * 1024),
-        name='second_experts',
-    )(e_a, gath_b, metas, w1, w3, w2, metas, hid_a, hid_b)
+        ] + gather_scratch([hid, meta], num_dev, sub_size) + gather_scratch([hid], num_dev, sub_size),
+        compiler_params=pltpu.CompilerParams(collective_id=1, has_side_effects=True, vmem_limit_bytes=VMEM_CAP),
+        name='run_layer',
+    )(q, k, v, x_a, x_b, w_out, meta, w1, w3, w2, gain)
 
 
 def solution(mesh):
@@ -430,16 +476,13 @@
         exp_local = w_gate.shape[0]
         num_exp = exp_local * num_dev
         tok_count, top_k = route_idx.shape[1:]
-        dim = input_a.shape[2]
         cap_slots = 3 * top_k * tok_count // (2 * num_exp)
 
         meta = jnp.concatenate([jnp.stack([slot_codes(route_idx[m], num_exp, cap_slots) for m in range(2)]), route_gate], axis=2)
         meta = meta.transpose(0, 2, 1)
-        hidden = [attention_block(x, attn_norm, w_query, w_key, w_value, w_out).reshape(tok_count, dim) for x in (input_a, input_b)]
-        normed = [rms_norm(h, moe_norm) for h in hidden]
-        gath_a, metas = gather_tokens([normed[0], meta], num_dev, sub_size, 1)
-        gath_b, _, e_a = first_experts(normed[1], gath_a, metas, w_gate, w_up, w_down, cap_slots, sub_size, 2)
-        outs = second_experts(e_a, gath_b, metas, w_gate, w_up, w_down, hidden[0], hidden[1], sub_size, 3)
+        normed = rms_norm(jnp.concatenate([input_a, input_b]), attn_norm)
+        q, k, v = [jnp.einsum('bsd,dhc->bhsc', normed, w, preferred_element_type=jnp.float32).astype(jnp.bfloat16) for w in (w_query, w_key, w_value)]
+        outs = run_layer(q, k, v, input_a, input_b, w_out.reshape(-1, w_out.shape[2]), meta, w_gate, w_up, w_down, moe_norm[None, :], num_dev, cap_slots, sub_size)
         return outs[0].reshape(input_a.shape), outs[1].reshape(input_b.shape)
 
     return jax.shard_map(device_body, mesh=mesh, in_specs=(tok_spec, tok_spec, route_spec, route_spec, P(), P(), P(), P(), P(), P(), exp_spec, exp_spec, exp_spec), out_specs=(tok_spec, tok_spec), check_vma=False)

time: 607 us -> 563 us (0.928)
  the two profiles are of different devices: /device:TPU:16 before, /device:TPU:0 now
where the time goes in v3:
time: 563 us; the launch traced here: 558 us
  Pallas kernels  522 us (93%)
  matrix products  25.4 us (5%)
    pallas_call x1, Pallas kernels, run_layer(): pl.pallas_call(functools.partial(layer_body, sub_size), out_shape=[hid, h...  522 us
    dot_general x3, matrix products, device_body(): jnp.einsum('bsd,dhc->bhsc', normed, w, preferred_element_type=jnp.float32)  25.1 us

profile of v3, /device:TPU:0, one launch (start us, length us, event | category | flops | bytes accessed | tf_op | source)
XLA Modules:
  0.0 557.8 jit_solution(14574426718154011866)
XLA Ops:
  0.6 2.0 fusion.9
  2.7 0.7 slice_bitcast_fusion.1
  3.4 0.1 fusion.20
  3.5 0.1 fusion.19
  3.5 0.0 slice-start
  3.5 0.2 fusion.21
  3.7 0.2 fusion.22
  3.9 0.2 select_reduce_fusion
  4.1 1.0 bitcast_add_fusion.1
  5.1 1.3 maximum_bitcast_fusion.meta
  6.4 0.0 slice-start.2
  6.4 10.0 %convert_bitcast_fusion.1.k = bf16[2,16,256,128]{3,2,1,0:T(8,128)(2,1)} fusion(bf16[2048,16,128]{2,1,0:T(8,128)(2,1)} %param.19, f32[2048]{0:T(1024)} %param.17, f32[2,256]{1,0:T(2,128)S(1)} %add_rsqrt_fusion, bf16[1,256,2048]{2,1,0:T(8,128)(2,1)} %x_b.1, bf16[1,256,2048]{2,1,0:T(8,128)(2,1)} %x_a.1), kind=kOutput, calls=%fused_computation.17 | convolution fusion | flops 4303355904 | bytes 12593152 | tf_op jit(solution)/shard_map/bsd,dhc->bhsc/dot_general | solution.py:484
  16.5 0.0 slice-done
  16.5 0.0 copy-done
  16.5 0.0 copy-done.1
  16.5 0.0 slice-done.1
  16.5 0.0 copy-done.2
  16.5 0.0 slice-start.3
  16.5 7.5 %convert_bitcast_fusion.v = bf16[2,16,256,128]{3,2,1,0:T(8,128)(2,1)} fusion(bf16[2048,16,128]{2,1,0:T(8,128)(2,1)S(1)} %bitcast.49, f32[2048]{0:T(1024)S(1)} %copy-done.2, f32[2,256]{1,0:T(2,128)S(1)} %add_rsqrt_fusion, bf16[1,256,2048]{2,1,0:T(8,128)(2,1)S(1)} %copy-done, bf16[1,256,2048]{2,1,0:T(8,128)(2,1)S(1)} %copy-done.1), kind=kOutput, calls=%fused_computation.16 | convolution fusion | flops 4303355904 | bytes 12593152 | tf_op jit(solution)/shard_map/bsd,dhc->bhsc/dot_general | solution.py:484
  24.0 0.0 slice-done.3
  24.0 7.5 %convert_bitcast_fusion.2.q = bf16[2,16,256,128]{3,2,1,0:T(8,128)(2,1)} fusion(bf16[2048,16,128]{2,1,0:T(8,128)(2,1)S(1)} %bitcast.51, f32[2048]{0:T(1024)S(1)} %copy-done.2, f32[2,256]{1,0:T(2,128)S(1)} %add_rsqrt_fusion, bf16[1,256,2048]{2,1,0:T(8,128)(2,1)S(1)} %copy-done, bf16[1,256,2048]{2,1,0:T(8,128)(2,1)S(1)} %copy-done.1), kind=kOutput, calls=%fused_computation.18 | convolution fusion | flops 4303355904 | bytes 12593152 | tf_op jit(solution)/shard_map/bsd,dhc->bhsc/dot_general | solution.py:484
  31.5 521.7 %run_layer.1 = (bf16[256,2048]{1,0:T(8,128)(2,1)}, bf16[256,2048]{1,0:T(8,128)(2,1)}, bf16[16,256,2048]{2,1,0:T(8,128)(2,1)}, bf16[16,256,2048]{2,1,0:T(8,128)(2...) custom-call(bf16[2,16,256,128]{3,2,1,0:T(8,128)(2,1)} %convert_bitca, ...), custom_call_target="tpu_custom_call" | custom-call | tf_op jit(solution)/shard_map/run_layer/pallas_call | solution.py:444
  553.2 2.3 copy.46
  555.5 2.3 copy.47
  (8 shorter events, 0.0 us)
Async XLA Ops:
  3.5 12.9 %slice-start = ((s8[8388608]{0:T(1024)(128)(4,1)}), s8[4194304]{0:T(1024)(128)(4,1)S(1)}, s32[]{:S(2)}) async-start(s8[8388608]{0:T(1024)(128)(4,1)} %bitcast.48), calls=%async_computation | async-start | bytes 8388608
  6.4 10.1 %copy-start = (bf16[1,256,2048]{2,1,0:T(8,128)(2,1)S(1)}, bf16[1,256,2048]{2,1,0:T(8,128)(2,1)}, u32[]{:S(2)}) copy-start(bf16[1,256,2048]{2,1,0:T(8,128)(2,1)} %x_b.1) | copy-start | bytes 3145732
  6.4 10.1 %copy-start.1 = (bf16[1,256,2048]{2,1,0:T(8,128)(2,1)S(1)}, bf16[1,256,2048]{2,1,0:T(8,128)(2,1)}, u32[]{:S(2)}) copy-start(bf16[1,256,2048]{2,1,0:T(8,128)(2,1)} %x_a.1) | copy-start | bytes 3145732
  6.4 10.1 %slice-start.1 = ((s8[8388608]{0:T(1024)(128)(4,1)}), s8[4194304]{0:T(1024)(128)(4,1)S(1)}, s32[]{:S(2)}) async-start(s8[8388608]{0:T(1024)(128)(4,1)} %bitcast.48), calls=%async_computation.1 | async-start | bytes 8388608
  6.4 10.1 %copy-start.2 = (f32[2048]{0:T(1024)S(1)}, f32[2048]{0:T(1024)}, u32[]{:S(2)}) copy-start(f32[2048]{0:T(1024)} %param.17) | copy-start | bytes 24580
  6.4 17.6 %slice-start.2 = ((s8[8388608]{0:T(1024)(128)(4,1)}), s8[4194304]{0:T(1024)(128)(4,1)S(1)}, s32[]{:S(2)}) async-start(s8[8388608]{0:T(1024)(128)(4,1)} %bitcast.50), calls=%async_computation.2 | async-start | bytes 8388608
  16.5 7.5 %slice-start.3 = ((s8[8388608]{0:T(1024)(128)(4,1)}), s8[4194304]{0:T(1024)(128)(4,1)S(1)}, s32[]{:S(2)}) async-start(s8[8388608]{0:T(1024)(128)(4,1)} %bitcast.50), calls=%async_computation.3 | async-start | bytes 8388608

commit v4 on v3

--- a/solution.py
+++ b/solution.py
@@ -96,8 +96,8 @@
 
 
 class Gather:
-    def __init__(self, sub_size, ins, outs, stage, recv, right_s, left_s, far_s, core_s, loc):
-        self.count, self.sub_size = len(ins), sub_size
+    def __init__(self, sub_size, ins, outs, stage, entries, recv, right_s, left_s, far_s, core_s, loc):
+        self.sub_size, self.entries = sub_size, entries
         self.ins, self.outs, self.stage = ins, outs, stage
         self.recv, self.right_s, self.left_s, self.far_s, self.core_s, self.loc = recv, right_s, left_s, far_s, core_s, loc
         ep, sub = lax.axis_index('ep'), lax.axis_index('sub')
@@ -109,104 +109,139 @@
         self.to_right, self.to_left = {'ep': ep, 'sub': sub + 1}, {'ep': ep, 'sub': sub - 1}
         self.to_far, self.to_core = {'ep': self.ep_far, 'sub': sub}, {'ep': self.ep_core, 'sub': sub}
 
-    def copies(self, src, blk, sem, slot, dev):
-        return [pltpu.make_async_remote_copy(src_ref=src(a), dst_ref=self.outs[a].at[blk], send_sem=sem.at[a, slot], recv_sem=self.recv.at[a, blk], device_id=dev, device_id_type=MESH) for a in range(self.count)]
-
-    def start(self, *args):
-        for cp in self.copies(*args):
-            cp.start()
-
-    def landed(self, blk):
-        for cp in self.copies(lambda a: self.outs[a].at[blk], blk, self.far_s, 0, self.to_far):
-            cp.wait_recv()
-
-    def sent(self, sem, slot, dev):
-        for cp in self.copies(lambda a: self.outs[a].at[self.me], 0, sem, slot, dev):
-            cp.wait_send()
+    def copy(self, n, blk, sem, slot, dev):
+        a, first, rows, _ = self.entries[n]
+        ref = self.outs[a].at[blk, pl.ds(first, rows)]
+        return pltpu.make_async_remote_copy(src_ref=ref, dst_ref=ref, send_sem=sem.at[n, slot], recv_sem=self.recv.at[n, blk], device_id=dev, device_id_type=MESH)
+
+    def right(self, n, blk, slot):
+        pl.when(self.sub < self.last)(lambda: self.copy(n, blk, self.right_s, slot, self.to_right).start())
+
+    def left(self, n, blk, slot):
+        pl.when(self.sub > 0)(lambda: self.copy(n, blk, self.left_s, slot, self.to_left).start())
+
+    def each(self, fn):
+        for n, entry in enumerate(self.entries):
+            fn(n, entry[3] == 'far')
 
     def begin(self):
         sub, me = self.sub, self.me
-        own = lambda a: self.outs[a].at[me]
-        for a in range(self.count):
-            if self.ins[a] is not None:
-                cp = pltpu.make_async_copy(self.ins[a], self.stage[a], self.loc.at[a])
+        for a, src in enumerate(self.ins):
+            if src is not None:
+                cp = pltpu.make_async_copy(src, self.stage[a], self.loc.at[a])
                 cp.start()
                 cp.wait()
-        keep = [pltpu.make_async_copy(self.stage[a], own(a), self.loc.at[a]) for a in range(self.count)]
+        keep = [pltpu.make_async_copy(self.stage[a], self.outs[a].at[me], self.loc.at[a]) for a in range(len(self.ins))]
         for cp in keep:
             cp.start()
         for cp in keep:
             cp.wait()
-        pl.when(sub < self.last)(lambda: self.start(own, me, self.right_s, sub, self.to_right))
-        pl.when(sub > 0)(lambda: self.start(own, me, self.left_s, sub, self.to_left))
-        self.start(own, me, self.far_s, sub, self.to_far)
-        self.start(own, me, self.core_s, sub, self.to_core)
-
-    def from_far(self, src_sub):
+
+        def own(n, far):
+            self.copy(n, me, self.far_s, sub, self.to_far).start()
+            self.right(n, me, sub)
+            self.left(n, me, sub)
+            self.copy(n, me, self.core_s, sub, self.to_core).start()
+
+        for n, entry in enumerate(self.entries):
+            if entry[3] == 'far':
+                own(n, True)
+        for n, entry in enumerate(self.entries):
+            if entry[3] == 'line':
+                own(n, False)
+
+    def from_near(self, src_sub, send):
+        blk = self.ep * self.sub_size + src_sub
+
+        def one(n, far):
+            self.copy(n, blk, self.far_s, 0, self.to_far).wait_recv()
+            send(n, blk, src_sub)
+            if not far:
+                self.copy(n, blk, self.far_s, src_sub, self.to_far).start()
+            self.copy(n, blk, self.core_s, src_sub, self.to_core).start()
+
+        self.each(one)
+
+    def from_far(self, src_sub, sends):
         blk = self.ep_far * self.sub_size + src_sub
-        self.landed(blk)
-        self.start(lambda a: self.outs[a].at[blk], blk, self.core_s, self.sub_size + src_sub, self.to_core)
-
-    def from_line(self, src_sub, sem, cond, dev):
-        blk = self.ep * self.sub_size + src_sub
-        src = lambda a: self.outs[a].at[blk]
-        self.landed(blk)
-        pl.when(cond)(lambda: self.start(src, blk, sem, src_sub, dev))
-        self.start(src, blk, self.far_s, src_sub, self.to_far)
-        self.start(src, blk, self.core_s, src_sub, self.to_core)
+        slot = self.sub_size + src_sub
+
+        def one(n, far):
+            self.copy(n, blk, self.far_s, 0, self.to_far).wait_recv()
+            if far:
+                for send in sends:
+                    send(n, blk, slot)
+            self.copy(n, blk, self.core_s, slot, self.to_core).start()
+
+        self.each(one)
+
+    def far_pair(self, dist):
+        sub, last = self.sub, self.last
+        pl.when(sub - dist >= 0)(lambda: self.from_far(sub - dist, [self.right]))
+        pl.when(sub + dist <= last)(lambda: self.from_far(sub + dist, [self.left]))
 
     def hop(self, dist):
         sub, last = self.sub, self.last
-        pl.when(sub - dist >= 0)(lambda: self.from_line(sub - dist, self.right_s, sub < last, self.to_right))
-        pl.when(sub + dist <= last)(lambda: self.from_line(sub + dist, self.left_s, sub > 0, self.to_left))
+        pl.when(sub - dist >= 0)(lambda: self.from_near(sub - dist, self.right))
+        pl.when(sub + dist <= last)(lambda: self.from_near(sub + dist, self.left))
         if dist == 1:
-            self.from_far(sub)
+            self.from_far(sub, [self.right, self.left])
         else:
-            pl.when(sub - dist + 1 >= 0)(lambda: self.from_far(sub - dist + 1))
-            pl.when(sub + dist - 1 <= last)(lambda: self.from_far(sub + dist - 1))
+            self.far_pair(dist - 1)
 
     def core_ready(self, first, stop):
         for k in range(first, stop):
             src_sub = at_rank(self.sub, k)
-            self.landed(self.ep_core * self.sub_size + src_sub)
-            self.landed(self.ep_diag * self.sub_size + src_sub)
+            for ep in (self.ep_core, self.ep_diag):
+                self.each(lambda n, far: self.copy(n, ep * self.sub_size + src_sub, self.far_s, 0, self.to_far).wait_recv())
 
     def last_far(self):
-        sub, last = self.sub, self.last
-        pl.when(sub - last >= 0)(lambda: self.from_far(sub - last))
-        pl.when(sub + last <= last)(lambda: self.from_far(sub + last))
+        self.far_pair(self.last)
 
     def drain(self):
         sub, last, size = self.sub, self.last, self.sub_size
-        for src_sub in range(size):
-            self.sent(self.far_s, src_sub, self.to_far)
-            self.sent(self.core_s, src_sub, self.to_core)
-            self.sent(self.core_s, size + src_sub, self.to_core)
-            pl.when((sub >= src_sub) & (sub < last))(lambda: self.sent(self.right_s, src_sub, self.to_right))
-            pl.when((sub <= src_sub) & (sub > 0))(lambda: self.sent(self.left_s, src_sub, self.to_left))
-
-
-def gather_scratch(arrays, num_dev, sub_size):
-    sems = lambda n: pltpu.SemaphoreType.DMA((len(arrays), n))
-    return [pltpu.VMEM(a.shape, a.dtype) for a in arrays] + [sems(num_dev), sems(sub_size), sems(sub_size), sems(sub_size), sems(2 * sub_size), pltpu.SemaphoreType.DMA((len(arrays),))]
+
+        def one(n, far):
+            sent = lambda sem, slot: self.copy(n, 0, sem, slot, self.to_far).wait_send()
+            for src in range(size):
+                sent(self.core_s, src)
+                sent(self.core_s, size + src)
+                if not far:
+                    sent(self.far_s, src)
+                for slot in ((src, size + src) if far else (src,)):
+                    pl.when((sub >= src) & (sub < last))(lambda: sent(self.right_s, slot))
+                    pl.when((sub <= src) & (sub > 0))(lambda: sent(self.left_s, slot))
+            if far:
+                sent(self.far_s, sub)
+
+        self.each(one)
+
+
+def gather_scratch(arrays, entries, num_dev, sub_size):
+    sems = lambda n: pltpu.SemaphoreType.DMA((len(entries), n))
+    return [pltpu.VMEM(a.shape, a.dtype) for a in arrays] + [sems(num_dev)] + [sems(2 * sub_size) for _ in range(4)] + [pltpu.SemaphoreType.DMA((len(arrays),))]
+
+
+def split_rows(rows, first_far):
+    return [(0, 0, first_far, 'line'), (0, first_far, rows - first_far, 'far')]
 
 
 FFN_STEPS = 4
-
-
-HALVES = 2
-
-
-def pick_rows(mb, half, ep, sub, sub_size, gath, metas, rows, exp_local, cap_slots):
+SPLIT = 1
+LINE_ROWS_A = 208
+LINE_ROWS_B = 208
+
+
+def pick_rows(mb, first, ranks, ep, sub, sub_size, gath, metas, rows, exp_local, cap_slots):
     num_dev, tok_count, dim = gath.shape
     top_k = metas.shape[2] // 2
     room = exp_local * cap_slots
-    blocks = num_dev // HALVES
     ep_size = num_dev // sub_size
+    blocks = ranks * ep_size
     base = ((ep * sub_size + sub) * room).astype(jnp.float32)
 
     def block(p):
-        q = half * blocks + p
+        q = first * ep_size + p
         return (q % ep_size) * sub_size + at_rank(sub, q // ep_size)
 
     def pick(code_ref, tok_ref, out_ref):
@@ -223,7 +258,7 @@
         pick,
         grid=(blocks,),
         in_specs=[pl.BlockSpec((1, 1) + metas.shape[2:], lambda p: (block(p), mb, 0, 0)), pl.BlockSpec((1, tok_count, dim), lambda p: (block(p), 0, 0))],
-        out_specs=[pl.BlockSpec((exp_local, cap_slots, dim), lambda p: (0, half * blocks + p, 0))],
+        out_specs=[pl.BlockSpec((exp_local, cap_slots, dim), lambda p: (0, first * ep_size + p, 0))],
     )(metas, gath, rows)
 
 
@@ -238,16 +273,17 @@
 
         @pl.when(step < steps)
         def _():
-            x = x_ref[0]
-            gate_h = jnp.dot(x, w1_ref[0], preferred_element_type=jnp.float32)
-            up_h = jnp.dot(x, w3_ref[0], preferred_element_type=jnp.float32)
-            act_ref[step] = (jax.nn.silu(gate_h) * up_h).astype(jnp.bfloat16)
+            cols = pl.ds(pl.multiple_of(step * ft, ft), ft)
+            for m in range(SPLIT):
+                part = pl.ds(m * (act_ref.shape[0] // SPLIT), act_ref.shape[0] // SPLIT)
+                x = x_ref[0, part, :]
+                gate_h = jnp.dot(x, w1_ref[0], preferred_element_type=jnp.float32)
+                up_h = jnp.dot(x, w3_ref[0], preferred_element_type=jnp.float32)
+                act_ref[part, cols] = (jax.nn.silu(gate_h) * up_h).astype(jnp.bfloat16)
 
         @pl.when(step >= steps)
         def _():
-            acc = jnp.dot(act_ref[0], w2_ref[0, 0:ft, :], preferred_element_type=jnp.float32)
-            for k in range(1, steps):
-                acc = acc + jnp.dot(act_ref[k], w2_ref[0, k * ft:(k + 1) * ft, :], preferred_element_type=jnp.float32)
+            acc = jnp.dot(act_ref[...], w2_ref[0], preferred_element_type=jnp.float32)
             out_ref[...] = acc.astype(jnp.bfloat16).reshape(out_ref.shape)
 
         hook(e, step)
@@ -266,7 +302,7 @@
     )(rows, w1, w3, w2, e_out)
 
 
-PARTS = 2
+PARTS = 4
 
 
 class Combine:
@@ -371,11 +407,11 @@
             pl.when(dst != self.sub)(lambda: self.line_copy(dst, h, dst, self.to_right).wait_send())
 
 
-def layer_body(sub_size, q, k, v, x_a, x_b, w_out, meta, w1, w3, w2, gain, out_a, out_b, gath_a, gath_b, metas, rows_a, rows_b, e_a, e_b, land_a, land_b,
+def layer_body(sub_size, entries_a, entries_b, q, k, v, x_a, x_b, w_out, meta, w1, w3, w2, gain, out_a, out_b, gath_a, gath_b, metas, rows_a, rows_b, e_a, e_b, land_a, land_b,
                act_ref, near_meta, hid_a, hid_b, x_sem, inbox, sums, mix, tile, meta_sem, a_recv, a_send, z_recv, z_send, loads, stage_a, stage_m, *rest):
     sems_a, stage_b, sems_b = rest[:6], rest[6], rest[7:]
-    ga = Gather(sub_size, [None, meta], [gath_a, metas], [stage_a, stage_m], *sems_a)
-    gb = Gather(sub_size, [None], [gath_b], [stage_b], *sems_b)
+    ga = Gather(sub_size, [None, meta], [gath_a, metas], [stage_a, stage_m], entries_a, *sems_a)
+    gb = Gather(sub_size, [None], [gath_b], [stage_b], entries_b, *sems_b)
     sems = (a_recv, a_send, z_recv, z_send, loads)
     ca = Combine(0, sub_size, e_a, near_meta, hid_a, out_a, land_a, inbox, sums, mix, tile, *sems)
     cb = Combine(1, sub_size, e_b, near_meta, hid_b, out_b, land_b, inbox, sums, mix, tile, *sems)
@@ -386,15 +422,15 @@
     def at(e, step, when_e, when_step, fn):
         pl.when((e == when_e) & (step == when_step))(fn)
 
-    def pick(mb, half):
-        pick_rows(mb, half, ep, sub, sub_size, (gath_a, gath_b)[mb], metas, (rows_a, rows_b)[mb], w1.shape[0], e_a.shape[2])
+    def pick(mb, first, ranks):
+        pick_rows(mb, first, ranks, ep, sub, sub_size, (gath_a, gath_b)[mb], metas, (rows_a, rows_b)[mb], w1.shape[0], e_a.shape[2])
 
     def hook_a(e, step):
-        at(e, step, 0, 0, lambda: gb.hop(2))
-        at(e, step, 1, 4, lambda: gb.hop(3))
+        at(e, step, 0, 7, lambda: gb.hop(2))
+        at(e, step, 2, 4, lambda: gb.hop(3))
 
     def hook_b(e, step):
-        pl.when(step == 2 * FFN_STEPS - 1)(lambda: ca.event(e + 1))
+        pl.when(step % FFN_STEPS == FFN_STEPS - 1)(lambda: ca.event(2 + 2 * e + step // FFN_STEPS))
 
     ca.greet()
     attend(0, q, k, v, x_a, w_out, gain, hid_a, stage_a, x_sem)
@@ -403,27 +439,30 @@
     ga.hop(1)
     ga.hop(2)
     ga.core_ready(0, 2)
-    pick(0, 0)
+    pick(0, 0, 2)
     ga.hop(3)
     gb.begin()
+    ga.core_ready(2, 3)
+    pick(0, 2, 1)
     ga.last_far()
-    ga.core_ready(2, 4)
+    ga.core_ready(3, 4)
+    pick(0, 3, 1)
     gb.hop(1)
-    pick(0, 1)
     run_experts(*weights, rows_a, e_a, act_ref, hook_a)
     ca.begin()
     pull = pltpu.make_async_copy(metas.at[pl.ds(ep * sub_size, sub_size)], near_meta, meta_sem)
     pull.start()
     pull.wait()
     gb.core_ready(0, 2)
-    pick(1, 0)
     gb.last_far()
+    pick(1, 0, 2)
+    ca.event(0)
     gb.core_ready(2, 4)
-    pick(1, 1)
-    ca.event(0)
+    pick(1, 2, 2)
+    ca.event(1)
     run_experts(*weights, rows_b, e_b, act_ref, hook_b)
     cb.begin()
-    pl.loop(w1.shape[0] + 1, events)(ca.event)
+    pl.loop(2 + 2 * w1.shape[0], events)(ca.event)
     ca.end()
     pl.loop(0, events)(cb.event)
     cb.end()
@@ -441,13 +480,15 @@
     land = bf(sub_size, 4, exp_local, cap_slots, dim)
     rows, e_out = bf(exp_local, num_dev * cap_slots, dim), bf(num_dev, exp_local, cap_slots, dim)
     vmem = pl.BlockSpec(memory_space=pltpu.VMEM)
+    entries_a = split_rows(tok_count, LINE_ROWS_A) + [(1, 0, meta.shape[0], 'line')]
+    entries_b = split_rows(tok_count, LINE_ROWS_B)
     return pl.pallas_call(
-        functools.partial(layer_body, sub_size),
+        functools.partial(layer_body, sub_size, entries_a, entries_b),
         out_shape=[hid, hid, gath, gath, jax.ShapeDtypeStruct((num_dev,) + meta.shape, meta.dtype), rows, rows, e_out, e_out, land, land],
         in_specs=[ANY] * 10 + [vmem],
         out_specs=[vmem] * 2 + [ANY] * 9,
         scratch_shapes=[
-            pltpu.VMEM((FFN_STEPS, num_dev * cap_slots, ff // FFN_STEPS), jnp.bfloat16),
+            pltpu.VMEM((num_dev * cap_slots, ff), jnp.bfloat16),
             pltpu.VMEM((sub_size,) + meta.shape, meta.dtype),
             pltpu.VMEM((tok_count, dim), jnp.bfloat16),
             pltpu.VMEM((tok_count, dim), jnp.bfloat16),
@@ -458,7 +499,7 @@
             pltpu.VMEM((4, exp_local, cap_slots, dim // PARTS), jnp.bfloat16),
             pltpu.SemaphoreType.DMA,
             dma(2, sub_size, 4, PARTS), dma(2, sub_size, 3, PARTS), dma(2, sub_size + 1, PARTS), dma(2, sub_size, PARTS), dma(4),
-        ] + gather_scratch([hid, meta], num_dev, sub_size) + gather_scratch([hid], num_dev, sub_size),
+        ] + gather_scratch([hid, meta], entries_a, num_dev, sub_size) + gather_scratch([hid], entries_b, num_dev, sub_size),
         compiler_params=pltpu.CompilerParams(collective_id=1, has_side_effects=True, vmem_limit_bytes=VMEM_CAP),
         name='run_layer',
     )(q, k, v, x_a, x_b, w_out, meta, w1, w3, w2, gain)

time: 563 us -> 536 us (0.952)
  Pallas kernels: 522 us -> 496 us
    pallas_call x1, Pallas kernels: 522 us -> 496 us  [run_layer(): pl.pallas_call(functools.partial(layer_body, sub_size, entries_a, entries...]
where the time goes in v4:
time: 536 us; the launch traced here: 533 us
  Pallas kernels  496 us (93%)
  matrix products  25.4 us (5%)
  local copies, waits for them, and re-layouts  5.37 us (1%)
    pallas_call x1, Pallas kernels, run_layer(): pl.pallas_call(functools.partial(layer_body, sub_size, entries_a, entries...  496 us
    dot_general x3, matrix products, device_body(): jnp.einsum('bsd,dhc->bhsc', normed, w, preferred_element_type=jnp.float32)  25.1 us

profile of v4, /device:TPU:0, one launch (start us, length us, event | category | flops | bytes accessed | tf_op | source)
XLA Modules:
  0.0 532.5 jit_solution(1161766318103782355)
XLA Ops:
  0.6 2.0 fusion.9
  2.7 0.7 slice_bitcast_fusion.1
  3.4 0.1 fusion.20
  3.5 0.1 fusion.19
  3.5 0.0 slice-start
  3.5 0.2 fusion.21
  3.7 0.2 fusion.22
  3.9 0.2 select_reduce_fusion
  4.1 1.0 bitcast_add_fusion.1
  5.1 1.3 maximum_bitcast_fusion.meta
  6.4 0.0 slice-start.2
  6.4 10.0 %convert_bitcast_fusion.1.k = bf16[2,16,256,128]{3,2,1,0:T(8,128)(2,1)} fusion(bf16[2048,16,128]{2,1,0:T(8,128)(2,1)} %param.19, f32[2048]{0:T(1024)} %param.17, f32[2,256]{1,0:T(2,128)S(1)} %add_rsqrt_fusion, bf16[1,256,2048]{2,1,0:T(8,128)(2,1)} %x_b.1, bf16[1,256,2048]{2,1,0:T(8,128)(2,1)} %x_a.1), kind=kOutput, calls=%fused_computation.17 | convolution fusion | flops 4303355904 | bytes 12593152 | tf_op jit(solution)/shard_map/bsd,dhc->bhsc/dot_general | solution.py:525
  16.5 0.0 slice-done
  16.5 0.0 copy-done
  16.5 0.0 copy-done.1
  16.5 0.0 slice-done.1
  16.5 0.0 copy-done.2
  16.5 0.0 slice-start.3
  16.5 7.5 %convert_bitcast_fusion.v = bf16[2,16,256,128]{3,2,1,0:T(8,128)(2,1)} fusion(bf16[2048,16,128]{2,1,0:T(8,128)(2,1)S(1)} %bitcast.49, f32[2048]{0:T(1024)S(1)} %copy-done.2, f32[2,256]{1,0:T(2,128)S(1)} %add_rsqrt_fusion, bf16[1,256,2048]{2,1,0:T(8,128)(2,1)S(1)} %copy-done, bf16[1,256,2048]{2,1,0:T(8,128)(2,1)S(1)} %copy-done.1), kind=kOutput, calls=%fused_computation.16 | convolution fusion | flops 4303355904 | bytes 12593152 | tf_op jit(solution)/shard_map/bsd,dhc->bhsc/dot_general | solution.py:525
  24.0 0.0 slice-done.2
  24.0 7.5 %convert_bitcast_fusion.2.q = bf16[2,16,256,128]{3,2,1,0:T(8,128)(2,1)} fusion(bf16[2048,16,128]{2,1,0:T(8,128)(2,1)S(1)} %bitcast.51, f32[2048]{0:T(1024)S(1)} %copy-done.2, f32[2,256]{1,0:T(2,128)S(1)} %add_rsqrt_fusion, bf16[1,256,2048]{2,1,0:T(8,128)(2,1)S(1)} %copy-done, bf16[1,256,2048]{2,1,0:T(8,128)(2,1)S(1)} %copy-done.1), kind=kOutput, calls=%fused_computation.18 | convolution fusion | flops 4303355904 | bytes 12593152 | tf_op jit(solution)/shard_map/bsd,dhc->bhsc/dot_general | solution.py:525
  31.5 496.4 %run_layer.1 = (bf16[256,2048]{1,0:T(8,128)(2,1)}, bf16[256,2048]{1,0:T(8,128)(2,1)}, bf16[16,256,2048]{2,1,0:T(8,128)(2,1)}, bf16[16,256,2048]{2,1,0:T(8,128)(2...) custom-call(bf16[2,16,256,128]{3,2,1,0:T(8,128)(2,1)} %convert_bitca, ...), custom_call_target="tpu_custom_call" | custom-call | tf_op jit(solution)/shard_map/run_layer/pallas_call | solution.py:485
  527.9 2.3 copy.46
  530.2 2.3 copy.47
  (8 shorter events, 0.0 us)
Async XLA Ops:
  3.5 12.9 %slice-start = ((s8[8388608]{0:T(1024)(128)(4,1)}), s8[4194304]{0:T(1024)(128)(4,1)S(1)}, s32[]{:S(2)}) async-start(s8[8388608]{0:T(1024)(128)(4,1)} %bitcast.48), calls=%async_computation | async-start | bytes 8388608
  6.4 10.1 %copy-start = (bf16[1,256,2048]{2,1,0:T(8,128)(2,1)S(1)}, bf16[1,256,2048]{2,1,0:T(8,128)(2,1)}, u32[]{:S(2)}) copy-start(bf16[1,256,2048]{2,1,0:T(8,128)(2,1)} %x_b.1) | copy-start | bytes 3145732
  6.4 10.1 %copy-start.1 = (bf16[1,256,2048]{2,1,0:T(8,128)(2,1)S(1)}, bf16[1,256,2048]{2,1,0:T(8,128)(2,1)}, u32[]{:S(2)}) copy-start(bf16[1,256,2048]{2,1,0:T(8,128)(2,1)} %x_a.1) | copy-start | bytes 3145732
  6.4 10.1 %slice-start.1 = ((s8[8388608]{0:T(1024)(128)(4,1)}), s8[4194304]{0:T(1024)(128)(4,1)S(1)}, s32[]{:S(2)}) async-start(s8[8388608]{0:T(1024)(128)(4,1)} %bitcast.48), calls=%async_computation.1 | async-start | bytes 8388608
  6.4 10.1 %copy-start.2 = (f32[2048]{0:T(1024)S(1)}, f32[2048]{0:T(1024)}, u32[]{:S(2)}) copy-start(f32[2048]{0:T(1024)} %param.17) | copy-start | bytes 24580
  6.4 17.6 %slice-start.2 = ((s8[8388608]{0:T(1024)(128)(4,1)}), s8[4194304]{0:T(1024)(128)(4,1)S(1)}, s32[]{:S(2)}) async-start(s8[8388608]{0:T(1024)(128)(4,1)} %bitcast.50), calls=%async_computation.2 | async-start | bytes 8388608
  16.5 7.5 %slice-start.3 = ((s8[8388608]{0:T(1024)(128)(4,1)}), s8[4194304]{0:T(1024)(128)(4,1)S(1)}, s32[]{:S(2)}) async-start(s8[8388608]{0:T(1024)(128)(4,1)} %bitcast.50), calls=%async_computation.3 | async-start | bytes 8388608
